TPU v7x, 128 devices: a whole 4x4x4 slice. The times are simulated.
128 devices in a mesh: gx: 4 (over x_lo, core), gy: 4 (over y), gz: 8 (over z, x_hi).
Axes of the slice: x: 4 (x_hi: 2, x_lo: 2; x = x_hi * 2 + x_lo), y: 4, z: 4, core: 2. Of those that a mesh axis runs over, the one named last changes fastest.
Arguments:
- orbitals: float32 [64, 32, 32, 1024], P(None, 'gx', 'gy', 'gz'), may hold values from -6 to 6
- potential: float32 [32, 32, 1024], P('gx', 'gy', 'gz'), may hold values from 0 to 0.5
- centre: float32 [64], replicated, may hold values from 3 to 5
- half_width: float32 [64], replicated, may hold values from 3 to 5
Outputs:
- filtered: float32 [64, 32, 32, 1024], P(None, 'gx', 'gy', 'gz')
All inputs are finite; a program needn't handle non-finite values.
Results may differ from a plain program's by a relative error of at most 0.00002.
Values sent between devices are 32-bit elements; how exact they have to be, the bound alone decides.
No kernel may reach another device: no remote copies, remote signals or barrier semaphores. Data moves between devices by JAX's collectives and lax.ppermute only.
A program may use at most 64 MiB of HBM per device.

v0:
```python
import jax
import jax.numpy as jnp
from jax import lax
from jax.sharding import PartitionSpec as P

shift_mass = 0.05
jacobi_weight = 2.0 / 3.0


def extended(array, sides, width):
    edges = {}
    for axis, dim in sides:
        size, length = (lax.axis_size(axis), array.shape[dim])
        up = [(i, (i + 1) % size) for i in range(size)]
        last = lax.slice_in_dim(array, length - width, length, axis=dim)
        leading = lax.slice_in_dim(array, 0, width, axis=dim)
        edges[dim] = (
            lax.ppermute(last, axis, up),
            lax.ppermute(leading, axis, [(b, a) for a, b in up]),
        )
    done = []
    for _, dim in sides:
        low, high = edges[dim]
        around = [(width, width) if d in done else (0, 0) for d in range(array.ndim)]
        array = jnp.concatenate([jnp.pad(low, around), array, jnp.pad(high, around)], axis=dim)
        done.append(dim)
    return array


def neighbour_sum(padded):
    total = padded[:, 2:, 1:-1, 1:-1] + padded[:, :-2, 1:-1, 1:-1]
    total = total + padded[:, 1:-1, 2:, 1:-1] + padded[:, 1:-1, :-2, 1:-1]
    return total + padded[:, 1:-1, 1:-1, 2:] + padded[:, 1:-1, 1:-1, :-2]


def restrict(field):
    shape = field.shape
    return 0.5 * field.reshape(shape[0], shape[1] // 2, 2, shape[2] // 2, 2, shape[3] // 2, 2).sum(
        axis=(2, 4, 6)
    )


def average_cells(field):
    shape = field.shape
    return 0.125 * field.reshape(shape[0] // 2, 2, shape[1] // 2, 2, shape[2] // 2, 2).sum(
        axis=(1, 3, 5)
    )


def prolong(field):
    return jnp.repeat(jnp.repeat(jnp.repeat(field, 2, 1), 2, 2), 2, 3)


def relax(level, source, diagonal, coupling, extend):
    applied = diagonal * level - coupling * neighbour_sum(extend(level))
    return level + jacobi_weight * (source - applied) / diagonal


def smooth_two(source, diagonal, extend):
    level = jacobi_weight * source / diagonal
    for sweep_index in range(2):
        level = relax(level, source, diagonal, 0.03125, extend)
    return level


def fine_apply(field, diagonal_fine):
    padded = extended(field, (("gx", 1), ("gy", 2), ("gz", 3)), 1)
    return diagonal_fine * field - 0.5 * neighbour_sum(padded)


def level_one_rim(field):
    return extended(field, (("gx", 1), ("gy", 2), ("gz", 3)), 1)


def level_two_rim(field):
    return extended(field, (("gx", 1), ("gy", 2), ("gz", 3)), 1)


def local(orbitals, potential, centre, half_width):
    middle = centre[:, None, None, None]
    spread = half_width[:, None, None, None]
    diagonal_fine = 3.0 + potential
    first_image = fine_apply(orbitals, diagonal_fine)
    first_order = (first_image - middle * orbitals) / spread
    second_image = fine_apply(first_order, diagonal_fine)
    second_order = 2.0 * (second_image - middle * first_order) / spread - orbitals
    potential_one = average_cells(potential)
    potential_two = average_cells(potential_one)
    diagonal_one = 0.75 + potential_one + shift_mass
    source_one = restrict(second_order)
    level_one = jacobi_weight * source_one / diagonal_one
    level_one = relax(level_one, source_one, diagonal_one, 0.125, level_one_rim)
    residue = source_one - (
        diagonal_one * level_one - 0.125 * neighbour_sum(level_one_rim(level_one))
    )
    source_two = restrict(residue)
    diagonal_two = 0.1875 + potential_two + shift_mass
    level_two = smooth_two(source_two, diagonal_two, level_two_rim)
    level_one = level_one + prolong(level_two)
    level_one = relax(level_one, source_one, diagonal_one, 0.125, level_one_rim)
    return second_order + prolong(level_one)


def solution(mesh):
    in_specs = (P(None, "gx", "gy", "gz"), P("gx", "gy", "gz"), P(), P())
    out_specs = P(None, "gx", "gy", "gz")
    return jax.shard_map(local, mesh=mesh, in_specs=in_specs, out_specs=out_specs, check_vma=False)
```

profile of v0, /device:TPU:1, one launch (start us, length us, event | category | flops | bytes accessed | tf_op | source)
XLA Modules:
  0.0 161.0 jit_solution(2832677705206226167)
XLA Ops:
  0.0 3.9 %copy.5 = f32[64,8,8,128]{0,3,2,1:T(8,128)} copy(f32[64,8,8,128]{3,2,1,0:T(8,128)} %param.4) | data formatting | bytes 4194304 | tf_op args[0]
  3.9 2.1 %fusion.91 = (f32[64,8,1,128]{0,3,2,1:T(8,128)}, f32[64,8,1,128]{0,3,2,1:T(8,128)S(1)}) fusion(f32[64,8,8,128]{0,3,2,1:T(8,128)} %copy.5), kind=kLoop, calls=%fused_computation.230 | loop fusion | bytes 1048576 | tf_op jit(solution)/shard_map/slice | solution.py:15
  6.0 3.6 %collective-permute-start.2 = (f32[64,8,1,128]{0,3,2,1:T(8,128)S(1)}, f32[64,8,1,128]{0,3,2,1:T(8,128)S(1)}, u32[]{:S(2)}, u32[]{:S(2)}) collective-permute-start(f32[64,8,1,128]{0,3,2,1:T(8,128)S(1)} %get-tuple-element.16), channel_id=1, source_target_pairs={{8,0},{16,8},{24,16},{0,24},{9,1},{17,9},{25,17},{1,25},{10,2},{18... | collective-permute-start | bytes 786440 | tf_op jit(solution)/shard_map/ppermute | solution.py:19
  9.5 2.3 %fusion.90 = (f32[64,1,8,128]{0,3,2,1:T(8,128)}, f32[64,1,8,128]{0,3,2,1:T(8,128)}) fusion(f32[64,8,8,128]{0,3,2,1:T(8,128)} %copy.5), kind=kLoop, calls=%fused_computation.229 | loop fusion | bytes 1048576 | tf_op jit(solution)/shard_map/slice | solution.py:15
  11.8 1.0 collective-permute-start
  12.8 1.1 collective-permute-start.1
  13.9 1.1 fusion.89
  15.0 6.0 %collective-permute-start.4 = (f32[64,8,8,1]{0,3,2,1:T(1,128)S(1)}, f32[64,8,8,1]{0,3,2,1:T(1,128)S(1)}, u32[]{:S(2)}, u32[]{:S(2)}) collective-permute-start(f32[64,8,8,1]{0,3,2,1:T(1,128)S(1)} %get-tuple-element.11), channel_id=1, source_target_pairs={{1,0},{2,1},{3,2},{4,3},{5,4},{6,5},{7,6},{0,7},{9,8},{10,9},{11,1... | collective-permute-start | bytes 49160 | tf_op jit(solution)/shard_map/ppermute | solution.py:19
  21.0 1.9 %collective-permute-start.5 = (f32[64,8,8,1]{0,3,2,1:T(1,128)S(1)}, f32[64,8,8,1]{0,3,2,1:T(1,128)S(1)}, u32[]{:S(2)}, u32[]{:S(2)}) collective-permute-start(f32[64,8,8,1]{0,3,2,1:T(1,128)S(1)} %get-tuple-element.12), channel_id=1, source_target_pairs={{0,1},{1,2},{2,3},{3,4},{4,5},{5,6},{6,7},{7,0},{8,9},{9,10},{10,1... | collective-permute-start | bytes 49160 | tf_op jit(solution)/shard_map/ppermute | solution.py:18
  22.9 2.1 %reshape.43 = f32[4,2,4,2,64,2]{5,4,3,2,1,0:T(8,128)S(1)} reshape(f32[8,8,128]{2,1,0:T(8,128)S(1)} %copy-done.3) | data formatting | bytes 65536 | tf_op jit(solution)/shard_map/reshape | solution.py:45
  25.0 0.2 reduce_sum.37
  25.2 1.1 pad.90
  26.3 1.1 pad.91
  27.4 2.0 %collective-permute-done.4 = f32[64,8,8,1]{0,3,2,1:T(1,128)S(1)} collective-permute-done((f32[64,8,8,1]{0,3,2,1:T(1,128)S(1)}, f32[64,8,8,1]{0,3,2,1:T(1,128)S(1)}, u32[]{:S(2)}, u32[]{:S(2)}) %collective-permute-start.4) | collective-permute-done | bytes 16416 | tf_op jit(solution)/shard_map/ppermute | solution.py:19
  29.4 3.9 %collective-permute-done.5 = f32[64,8,8,1]{0,3,2,1:T(1,128)S(1)} collective-permute-done((f32[64,8,8,1]{0,3,2,1:T(1,128)S(1)}, f32[64,8,8,1]{0,3,2,1:T(1,128)S(1)}, u32[]{:S(2)}, u32[]{:S(2)}) %collective-permute-start.5) | collective-permute-done | bytes 16416 | tf_op jit(solution)/shard_map/ppermute | solution.py:18
  33.4 14.0 %fusion.18 = f32[64,8,8,128]{0,3,2,1:T(8,128)S(1)} fusion(f32[64,8,8,1]{0,3,2,1:T(1,128)S(1)} %collective-permute-done.5, f32[64,10,1,128]{0,3,2,1:T(8,128)S(1)} %pad.90, f32[64,10,1,128]{0,3,2,1:T(8,128)S(1)} %pad.91, f32[64,1,8,128]{0,3,2,1:T(8,128)S(1)} %collective-permute-done, f32[64,8,8,128]{0,3,2,1:T(8,128)} %copy.5, ...), kind=kLoop, calls=%fused_computation.37 | loop fusion | flops 18350080 | bytes 5440000 | tf_op jit(solution)/shard_map/div | solution.py:84
  47.5 2.7 %collective-permute-start.8 = (f32[64,8,1,128]{0,3,2,1:T(8,128)S(1)}, f32[64,8,1,128]{0,3,2,1:T(8,128)S(1)}, u32[]{:S(2)}, u32[]{:S(2)}) collective-permute-start(f32[64,8,1,128]{0,3,2,1:T(8,128)S(1)} %get-tuple-element.10), channel_id=1, source_target_pairs={{8,0},{16,8},{24,16},{0,24},{9,1},{17,9},{25,17},{1,25},{10,2},{18... | collective-permute-start | bytes 786440 | tf_op jit(solution)/shard_map/ppermute | solution.py:19
  50.3 0.5 collective-permute-start.6
  50.8 1.3 collective-permute-start.7
  52.2 0.9 collective-permute-start.10
  53.1 8.2 %collective-permute-done.8 = f32[64,8,1,128]{0,3,2,1:T(8,128)S(1)} collective-permute-done((f32[64,8,1,128]{0,3,2,1:T(8,128)S(1)}, f32[64,8,1,128]{0,3,2,1:T(8,128)S(1)}, u32[]{:S(2)}, u32[]{:S(2)}) %collective-permute-start.8) | collective-permute-done | bytes 262176 | tf_op jit(solution)/shard_map/ppermute | solution.py:19
  61.4 3.2 %collective-permute-done.9 = f32[64,8,1,128]{0,3,2,1:T(8,128)S(1)} collective-permute-done((f32[64,8,1,128]{0,3,2,1:T(8,128)S(1)}, f32[64,8,1,128]{0,3,2,1:T(8,128)S(1)}, u32[]{:S(2)}, u32[]{:S(2)}) %collective-permute-start.9) | collective-permute-done | bytes 262176 | tf_op jit(solution)/shard_map/ppermute | solution.py:18
  64.7 3.0 %collective-permute-done.11 = f32[64,8,8,1]{0,3,2,1:T(1,128)S(1)} collective-permute-done((f32[64,8,8,1]{0,3,2,1:T(1,128)S(1)}, f32[64,8,8,1]{0,3,2,1:T(1,128)S(1)}, u32[]{:S(2)}, u32[]{:S(2)}) %collective-permute-start.11) | collective-permute-done | bytes 16416 | tf_op jit(solution)/shard_map/ppermute | solution.py:18
  67.7 11.8 %fusion.7 = f32[64,8,8,128]{0,3,2,1:T(8,128)} fusion(f32[64,8,8,128]{0,3,2,1:T(8,128)S(1)} %copy-done, f32[64,8,8,1]{0,3,2,1:T(1,128)S(1)} %collective-permute-done.11, f32[64,10,1,128]{0,3,2,1:T(8,128)S(1)} %pad.94, f32[64,10,1,128]{0,3,2,1:T(8,128)S(1)} %pad.95, f32[64,1,8,128]{0,3,2,1:T(8,128)S(1)} %collective-permute-done.6, ...), kind=kLoop, calls=%fused_computation.8 | loop fusion | flops 19398656 | bytes 7537152 | tf_op jit(solution)/shard_map/sub | solution.py:86
  79.5 4.8 %reduce_sum.36 = f32[64,4,4,64]{0,3,2,1:T(8,128)S(1)} reduce(f32[64,4,2,4,2,64,2]{0,6,5,4,3,2,1:T(2,128)} %bitcast.8, f32[]{:T(128)} %constant.11.clone.1), dimensions={2,4,6}, to_apply=%region_0.1 | reduce | flops 458752 | bytes 2359300 | tf_op jit(solution)/shard_map/reduce_sum | solution.py:38
  84.6 3.5 %collective-permute-start.14 = (f32[64,4,1,64]{0,3,2,1:T(8,128)S(1)}, f32[64,4,1,64]{0,3,2,1:T(8,128)S(1)}, u32[]{:S(2)}, u32[]{:S(2)}) collective-permute-start(f32[64,4,1,64]{0,3,2,1:T(8,128)S(1)} %get-tuple-element.34), channel_id=1, source_target_pairs={{8,0},{16,8},{24,16},{0,24},{9,1},{17,9},{25,17},{1,25},{10,2},{18... | collective-permute-start | bytes 196616 | tf_op jit(solution)/shard_map/ppermute | solution.py:19
  88.1 2.4 %collective-permute-start.12 = (f32[64,1,4,64]{0,3,2,1:T(8,128)S(1)}, f32[64,1,4,64]{0,3,2,1:T(8,128)S(1)}, u32[]{:S(2)}, u32[]{:S(2)}) collective-permute-start(f32[64,1,4,64]{0,3,2,1:T(8,128)S(1)} %get-tuple-element.32), channel_id=1, source_target_pairs={{32,0},{64,32},{96,64},{0,96},{33,1},{65,33},{97,65},{1,97},{34,2}... | collective-permute-start | bytes 196616 | tf_op jit(solution)/shard_map/ppermute | solution.py:19
  90.6 0.9 collective-permute-start.16
  91.5 2.2 %collective-permute-start.17 = (f32[64,4,4,1]{0,3,2,1:T(1,128)S(1)}, f32[64,4,4,1]{0,3,2,1:T(1,128)S(1)}, u32[]{:S(2)}, u32[]{:S(2)}) collective-permute-start(f32[64,4,4,1]{0,3,2,1:T(1,128)S(1)} %get-tuple-element.30), channel_id=1, source_target_pairs={{0,1},{1,2},{2,3},{3,4},{4,5},{5,6},{6,7},{7,0},{8,9},{9,10},{10,1... | collective-permute-start | bytes 12296 | tf_op jit(solution)/shard_map/ppermute | solution.py:18
  93.7 0.3 mul.166
  94.1 0.6 collective-permute-done.16
  94.7 2.9 %collective-permute-done.17 = f32[64,4,4,1]{0,3,2,1:T(1,128)S(1)} collective-permute-done((f32[64,4,4,1]{0,3,2,1:T(1,128)S(1)}, f32[64,4,4,1]{0,3,2,1:T(1,128)S(1)}, u32[]{:S(2)}, u32[]{:S(2)}) %collective-permute-start.17) | collective-permute-done | bytes 4128 | tf_op jit(solution)/shard_map/ppermute | solution.py:18
  97.6 0.4 fusion.54
  98.1 3.0 %collective-permute-start.20 = (f32[64,4,1,64]{0,3,2,1:T(8,128)S(1)}, f32[64,4,1,64]{0,3,2,1:T(8,128)S(1)}, u32[]{:S(2)}, u32[]{:S(2)}) collective-permute-start(f32[64,4,1,64]{0,3,2,1:T(8,128)S(1)} %get-tuple-element.28), channel_id=1, source_target_pairs={{8,0},{16,8},{24,16},{0,24},{9,1},{17,9},{25,17},{1,25},{10,2},{18... | collective-permute-start | bytes 196616 | tf_op jit(solution)/shard_map/ppermute | solution.py:19
  101.2 3.4 %collective-permute-start.18 = (f32[64,1,4,64]{0,3,2,1:T(8,128)S(1)}, f32[64,1,4,64]{0,3,2,1:T(8,128)S(1)}, u32[]{:S(2)}, u32[]{:S(2)}) collective-permute-start(f32[64,1,4,64]{0,3,2,1:T(8,128)S(1)} %get-tuple-element.26), channel_id=1, source_target_pairs={{32,0},{64,32},{96,64},{0,96},{33,1},{65,33},{97,65},{1,97},{34,2}... | collective-permute-start | bytes 196616 | tf_op jit(solution)/shard_map/ppermute | solution.py:19
  104.8 0.4 collective-permute-start.22
  105.3 2.5 %collective-permute-start.23 = (f32[64,4,4,1]{0,3,2,1:T(1,128)S(1)}, f32[64,4,4,1]{0,3,2,1:T(1,128)S(1)}, u32[]{:S(2)}, u32[]{:S(2)}) collective-permute-start(f32[64,4,4,1]{0,3,2,1:T(1,128)S(1)} %get-tuple-element.24), channel_id=1, source_target_pairs={{0,1},{1,2},{2,3},{3,4},{4,5},{5,6},{6,7},{7,0},{8,9},{9,10},{10,1... | collective-permute-start | bytes 12296 | tf_op jit(solution)/shard_map/ppermute | solution.py:18
  107.9 1.0 collective-permute-done.22
  108.8 2.5 %collective-permute-done.23 = f32[64,4,4,1]{0,3,2,1:T(1,128)S(1)} collective-permute-done((f32[64,4,4,1]{0,3,2,1:T(1,128)S(1)}, f32[64,4,4,1]{0,3,2,1:T(1,128)S(1)}, u32[]{:S(2)}, u32[]{:S(2)}) %collective-permute-start.23) | collective-permute-done | bytes 4128 | tf_op jit(solution)/shard_map/ppermute | solution.py:18
  111.4 0.4 fusion.41
  111.8 0.3 reduce_sum.38
  112.2 2.7 %collective-permute-start.26 = (f32[64,2,1,32]{0,3,2,1:T(8,128)S(1)}, f32[64,2,1,32]{0,3,2,1:T(8,128)S(1)}, u32[]{:S(2)}, u32[]{:S(2)}) collective-permute-start(f32[64,2,1,32]{0,3,2,1:T(8,128)S(1)} %get-tuple-element.46), channel_id=1, source_target_pairs={{8,0},{16,8},{24,16},{0,24},{9,1},{17,9},{25,17},{1,25},{10,2},{18... | collective-permute-start | bytes 49160 | tf_op jit(solution)/shard_map/ppermute | solution.py:19
  114.9 3.9 %collective-permute-start.24 = (f32[64,1,2,32]{0,3,2,1:T(8,128)S(1)}, f32[64,1,2,32]{0,3,2,1:T(8,128)S(1)}, u32[]{:S(2)}, u32[]{:S(2)}) collective-permute-start(f32[64,1,2,32]{0,3,2,1:T(8,128)S(1)} %get-tuple-element.44), channel_id=1, source_target_pairs={{32,0},{64,32},{96,64},{0,96},{33,1},{65,33},{97,65},{1,97},{34,2}... | collective-permute-start | bytes 49160 | tf_op jit(solution)/shard_map/ppermute | solution.py:19
  119.0 0.6 collective-permute-start.28
  119.6 2.4 %collective-permute-start.29 = (f32[64,2,2,1]{0,3,2,1:T(1,128)S(1)}, f32[64,2,2,1]{0,3,2,1:T(1,128)S(1)}, u32[]{:S(2)}, u32[]{:S(2)}) collective-permute-start(f32[64,2,2,1]{0,3,2,1:T(1,128)S(1)} %get-tuple-element.42), channel_id=1, source_target_pairs={{0,1},{1,2},{2,3},{3,4},{4,5},{5,6},{6,7},{7,0},{8,9},{9,10},{10,1... | collective-permute-start | bytes 3080 | tf_op jit(solution)/shard_map/ppermute | solution.py:18
  122.0 0.9 collective-permute-done.28
  122.9 2.7 %collective-permute-done.29 = f32[64,2,2,1]{0,3,2,1:T(1,128)S(1)} collective-permute-done((f32[64,2,2,1]{0,3,2,1:T(1,128)S(1)}, f32[64,2,2,1]{0,3,2,1:T(1,128)S(1)}, u32[]{:S(2)}, u32[]{:S(2)}) %collective-permute-start.29) | collective-permute-done | bytes 1056 | tf_op jit(solution)/shard_map/ppermute | solution.py:18
  125.7 2.7 %collective-permute-start.32 = (f32[64,2,1,32]{0,3,2,1:T(8,128)S(1)}, f32[64,2,1,32]{0,3,2,1:T(8,128)S(1)}, u32[]{:S(2)}, u32[]{:S(2)}) collective-permute-start(f32[64,2,1,32]{0,3,2,1:T(8,128)S(1)} %get-tuple-element.40), channel_id=1, source_target_pairs={{8,0},{16,8},{24,16},{0,24},{9,1},{17,9},{25,17},{1,25},{10,2},{18... | collective-permute-start | bytes 49160 | tf_op jit(solution)/shard_map/ppermute | solution.py:19
  128.5 2.9 %collective-permute-start.30 = (f32[64,1,2,32]{0,3,2,1:T(8,128)S(1)}, f32[64,1,2,32]{0,3,2,1:T(8,128)S(1)}, u32[]{:S(2)}, u32[]{:S(2)}) collective-permute-start(f32[64,1,2,32]{0,3,2,1:T(8,128)S(1)} %get-tuple-element.38), channel_id=1, source_target_pairs={{32,0},{64,32},{96,64},{0,96},{33,1},{65,33},{97,65},{1,97},{34,2}... | collective-permute-start | bytes 49160 | tf_op jit(solution)/shard_map/ppermute | solution.py:19
  131.6 2.9 %collective-permute-start.35 = (f32[64,2,2,1]{0,3,2,1:T(1,128)S(1)}, f32[64,2,2,1]{0,3,2,1:T(1,128)S(1)}, u32[]{:S(2)}, u32[]{:S(2)}) collective-permute-start(f32[64,2,2,1]{0,3,2,1:T(1,128)S(1)} %get-tuple-element.36), channel_id=1, source_target_pairs={{0,1},{1,2},{2,3},{3,4},{4,5},{5,6},{6,7},{7,0},{8,9},{9,10},{10,1... | collective-permute-start | bytes 3080 | tf_op jit(solution)/shard_map/ppermute | solution.py:18
  134.5 0.9 collective-permute-done.34
  135.4 2.2 %collective-permute-done.35 = f32[64,2,2,1]{0,3,2,1:T(1,128)S(1)} collective-permute-done((f32[64,2,2,1]{0,3,2,1:T(1,128)S(1)}, f32[64,2,2,1]{0,3,2,1:T(1,128)S(1)}, u32[]{:S(2)}, u32[]{:S(2)}) %collective-permute-start.35) | collective-permute-done | bytes 1056 | tf_op jit(solution)/shard_map/ppermute | solution.py:18
  138.1 3.0 %collective-permute-start.38 = (f32[64,4,1,64]{0,3,2,1:T(8,128)S(1)}, f32[64,4,1,64]{0,3,2,1:T(8,128)S(1)}, u32[]{:S(2)}, u32[]{:S(2)}) collective-permute-start(f32[64,4,1,64]{0,3,2,1:T(8,128)S(1)} %get-tuple-element.22), channel_id=1, source_target_pairs={{8,0},{16,8},{24,16},{0,24},{9,1},{17,9},{25,17},{1,25},{10,2},{18... | collective-permute-start | bytes 196616 | tf_op jit(solution)/shard_map/ppermute | solution.py:19
  141.1 3.1 %collective-permute-start.36 = (f32[64,1,4,64]{0,3,2,1:T(8,128)S(1)}, f32[64,1,4,64]{0,3,2,1:T(8,128)S(1)}, u32[]{:S(2)}, u32[]{:S(2)}) collective-permute-start(f32[64,1,4,64]{0,3,2,1:T(8,128)S(1)} %get-tuple-element.20), channel_id=1, source_target_pairs={{32,0},{64,32},{96,64},{0,96},{33,1},{65,33},{97,65},{1,97},{34,2}... | collective-permute-start | bytes 196616 | tf_op jit(solution)/shard_map/ppermute | solution.py:19
  144.5 2.9 %collective-permute-start.41 = (f32[64,4,4,1]{0,3,2,1:T(1,128)S(1)}, f32[64,4,4,1]{0,3,2,1:T(1,128)S(1)}, u32[]{:S(2)}, u32[]{:S(2)}) collective-permute-start(f32[64,4,4,1]{0,3,2,1:T(1,128)S(1)} %get-tuple-element.18), channel_id=1, source_target_pairs={{0,1},{1,2},{2,3},{3,4},{4,5},{5,6},{6,7},{7,0},{8,9},{9,10},{10,1... | collective-permute-start | bytes 12296 | tf_op jit(solution)/shard_map/ppermute | solution.py:18
  147.4 1.0 collective-permute-done.40
  148.4 2.2 %collective-permute-done.41 = f32[64,4,4,1]{0,3,2,1:T(1,128)S(1)} collective-permute-done((f32[64,4,4,1]{0,3,2,1:T(1,128)S(1)}, f32[64,4,4,1]{0,3,2,1:T(1,128)S(1)}, u32[]{:S(2)}, u32[]{:S(2)}) %collective-permute-start.41) | collective-permute-done | bytes 4128 | tf_op jit(solution)/shard_map/ppermute | solution.py:18
  150.6 0.4 fusion.31
  151.0 0.3 copy.17
  151.6 0.7 broadcast_in_dim.16
  152.3 0.3 broadcast_in_dim.17
  152.6 1.2 copy-done.1
  153.7 3.1 %copy_add_fusion = f32[64,8,8,128]{0,3,2,1:T(8,128)} fusion(f32[64,8,8,128]{0,3,2,1:T(8,128)S(1)} %copy-done.1, f32[64,8,8,128]{0,2,3,1:T(8,128)S(1)} %bitcast.9), kind=kLoop, calls=%fused_computation.62 | loop fusion | flops 524288 | bytes 6291456 | tf_op jit(solution)/shard_map/add | solution.py:101
  156.9 4.2 %copy.19 = f32[64,8,8,128]{3,2,1,0:T(8,128)} copy(f32[64,8,8,128]{0,3,2,1:T(8,128)} %copy_add_fusion) | data formatting | bytes 4194304 | tf_op jit(solution)/shard_map/add | solution.py:101
  (96 shorter events, 2.8 us)
Async XLA Ops:
  0.0 22.9 %copy-start.3 = (f32[8,8,128]{2,1,0:T(8,128)S(1)}, f32[8,8,128]{2,1,0:T(8,128)}, u32[]{:S(2)}) copy-start(f32[8,8,128]{2,1,0:T(8,128)} %param.5) | copy-start | bytes 98308
  6.0 15.0 %collective-permute-start.2 = (f32[64,8,1,128]{0,3,2,1:T(8,128)S(1)}, f32[64,8,1,128]{0,3,2,1:T(8,128)S(1)}, u32[]{:S(2)}, u32[]{:S(2)}) collective-permute-start(f32[64,8,1,128]{0,3,2,1:T(8,128)S(1)} %get-tuple-element.16), channel_id=1, source_target_pairs={{8,0},{16,8},{24,16},{0,24},{9,1},{17,9},{25,17},{1,25},{10,2},{18... | collective-permute-start | bytes 786440 | tf_op jit(solution)/shard_map/ppermute | solution.py:19
  9.5 23.8 %copy-start.4 = (f32[64]{0:T(128)S(1)}, f32[64]{0:T(128)}, u32[]{:S(2)}) copy-start(f32[64]{0:T(128)} %param.7) | copy-start | bytes 772
  9.5 23.9 %copy-start.5 = (f32[64]{0:T(128)S(1)}, f32[64]{0:T(128)}, u32[]{:S(2)}) copy-start(f32[64]{0:T(128)} %param.6) | copy-start | bytes 772
  9.5 16.8 %collective-permute-start.3 = (f32[64,8,1,128]{0,3,2,1:T(8,128)}, f32[64,8,1,128]{0,3,2,1:T(8,128)}, u32[]{:S(2)}, u32[]{:S(2)}) collective-permute-start(f32[64,8,1,128]{0,3,2,1:T(8,128)} %get-tuple-element.15), channel_id=1, source_target_pairs={{0,8},{8,16},{16,24},{24,0},{1,9},{9,17},{17,25},{25,1},{2,10},{10... | collective-permute-start | bytes 786440 | tf_op jit(solution)/shard_map/ppermute | solution.py:18
  11.8 21.5 %collective-permute-start = (f32[64,1,8,128]{0,3,2,1:T(8,128)}, f32[64,1,8,128]{0,3,2,1:T(8,128)S(1)}, u32[]{:S(2)}, u32[]{:S(2)}) collective-permute-start(f32[64,1,8,128]{0,3,2,1:T(8,128)} %get-tuple-element.14), channel_id=1, source_target_pairs={{32,0},{64,32},{96,64},{0,96},{33,1},{65,33},{97,65},{1,97},{34,2}... | collective-permute-start | bytes 786440 | tf_op jit(solution)/shard_map/ppermute | solution.py:19
  12.8 20.6 %collective-permute-start.1 = (f32[64,1,8,128]{0,3,2,1:T(8,128)}, f32[64,1,8,128]{0,3,2,1:T(8,128)S(1)}, u32[]{:S(2)}, u32[]{:S(2)}) collective-permute-start(f32[64,1,8,128]{0,3,2,1:T(8,128)} %get-tuple-element.13), channel_id=1, source_target_pairs={{0,32},{32,64},{64,96},{96,0},{1,33},{33,65},{65,97},{97,1},{2,34}... | collective-permute-start | bytes 786440 | tf_op jit(solution)/shard_map/ppermute | solution.py:18
  15.0 14.5 %collective-permute-start.4 = (f32[64,8,8,1]{0,3,2,1:T(1,128)S(1)}, f32[64,8,8,1]{0,3,2,1:T(1,128)S(1)}, u32[]{:S(2)}, u32[]{:S(2)}) collective-permute-start(f32[64,8,8,1]{0,3,2,1:T(1,128)S(1)} %get-tuple-element.11), channel_id=1, source_target_pairs={{1,0},{2,1},{3,2},{4,3},{5,4},{6,5},{7,6},{0,7},{9,8},{10,9},{11,1... | collective-permute-start | bytes 49160 | tf_op jit(solution)/shard_map/ppermute | solution.py:19
  21.0 1.9 %copy-start.2 = (f32[64,8,1,128]{0,3,2,1:T(8,128)}, f32[64,8,1,128]{0,3,2,1:T(8,128)S(1)}, u32[]{:S(2)}) copy-start(f32[64,8,1,128]{0,3,2,1:T(8,128)S(1)} %collective-permute-done.2) | copy-start | bytes 786436
  21.0 12.4 %collective-permute-start.5 = (f32[64,8,8,1]{0,3,2,1:T(1,128)S(1)}, f32[64,8,8,1]{0,3,2,1:T(1,128)S(1)}, u32[]{:S(2)}, u32[]{:S(2)}) collective-permute-start(f32[64,8,8,1]{0,3,2,1:T(1,128)S(1)} %get-tuple-element.12), channel_id=1, source_target_pairs={{0,1},{1,2},{2,3},{3,4},{4,5},{5,6},{6,7},{7,0},{8,9},{9,10},{10,1... | collective-permute-start | bytes 49160 | tf_op jit(solution)/shard_map/ppermute | solution.py:18
  47.4 20.3 %copy-start = (f32[64,8,8,128]{0,3,2,1:T(8,128)S(1)}, f32[64,8,8,128]{0,3,2,1:T(8,128)}, u32[]{:S(2)}) copy-start(f32[64,8,8,128]{0,3,2,1:T(8,128)} %copy.5) | copy-start | bytes 6291460
  47.5 13.8 %collective-permute-start.8 = (f32[64,8,1,128]{0,3,2,1:T(8,128)S(1)}, f32[64,8,1,128]{0,3,2,1:T(8,128)S(1)}, u32[]{:S(2)}, u32[]{:S(2)}) collective-permute-start(f32[64,8,1,128]{0,3,2,1:T(8,128)S(1)} %get-tuple-element.10), channel_id=1, source_target_pairs={{8,0},{16,8},{24,16},{0,24},{9,1},{17,9},{25,17},{1,25},{10,2},{18... | collective-permute-start | bytes 786440 | tf_op jit(solution)/shard_map/ppermute | solution.py:19
  50.3 14.3 %collective-permute-start.9 = (f32[64,8,1,128]{0,3,2,1:T(8,128)S(1)}, f32[64,8,1,128]{0,3,2,1:T(8,128)S(1)}, u32[]{:S(2)}, u32[]{:S(2)}) collective-permute-start(f32[64,8,1,128]{0,3,2,1:T(8,128)S(1)} %get-tuple-element.9), channel_id=1, source_target_pairs={{0,8},{8,16},{16,24},{24,0},{1,9},{9,17},{17,25},{25,1},{2,10},{10... | collective-permute-start | bytes 786440 | tf_op jit(solution)/shard_map/ppermute | solution.py:18
  50.3 17.4 %collective-permute-start.6 = (f32[64,1,8,128]{0,3,2,1:T(8,128)S(1)}, f32[64,1,8,128]{0,3,2,1:T(8,128)S(1)}, u32[]{:S(2)}, u32[]{:S(2)}) collective-permute-start(f32[64,1,8,128]{0,3,2,1:T(8,128)S(1)} %get-tuple-element.8), channel_id=1, source_target_pairs={{32,0},{64,32},{96,64},{0,96},{33,1},{65,33},{97,65},{1,97},{34,2}... | collective-permute-start | bytes 786440 | tf_op jit(solution)/shard_map/ppermute | solution.py:19
  50.8 16.9 %collective-permute-start.7 = (f32[64,1,8,128]{0,3,2,1:T(8,128)S(1)}, f32[64,1,8,128]{0,3,2,1:T(8,128)S(1)}, u32[]{:S(2)}, u32[]{:S(2)}) collective-permute-start(f32[64,1,8,128]{0,3,2,1:T(8,128)S(1)} %get-tuple-element.7), channel_id=1, source_target_pairs={{0,32},{32,64},{64,96},{96,0},{1,33},{33,65},{65,97},{97,1},{2,34}... | collective-permute-start | bytes 786440 | tf_op jit(solution)/shard_map/ppermute | solution.py:18
  52.2 12.4 %collective-permute-start.10 = (f32[64,8,8,1]{0,3,2,1:T(1,128)S(1)}, f32[64,8,8,1]{0,3,2,1:T(1,128)S(1)}, u32[]{:S(2)}, u32[]{:S(2)}) collective-permute-start(f32[64,8,8,1]{0,3,2,1:T(1,128)S(1)} %get-tuple-element.5), channel_id=1, source_target_pairs={{1,0},{2,1},{3,2},{4,3},{5,4},{6,5},{7,6},{0,7},{9,8},{10,9},{11,1... | collective-permute-start | bytes 49160 | tf_op jit(solution)/shard_map/ppermute | solution.py:19
  61.3 6.4 %collective-permute-start.11 = (f32[64,8,8,1]{0,3,2,1:T(1,128)S(1)}, f32[64,8,8,1]{0,3,2,1:T(1,128)S(1)}, u32[]{:S(2)}, u32[]{:S(2)}) collective-permute-start(f32[64,8,8,1]{0,3,2,1:T(1,128)S(1)} %get-tuple-element.6), channel_id=1, source_target_pairs={{0,1},{1,2},{2,3},{3,4},{4,5},{5,6},{6,7},{7,0},{8,9},{9,10},{10,1... | collective-permute-start | bytes 49160 | tf_op jit(solution)/shard_map/ppermute | solution.py:18
  84.6 6.9 %collective-permute-start.14 = (f32[64,4,1,64]{0,3,2,1:T(8,128)S(1)}, f32[64,4,1,64]{0,3,2,1:T(8,128)S(1)}, u32[]{:S(2)}, u32[]{:S(2)}) collective-permute-start(f32[64,4,1,64]{0,3,2,1:T(8,128)S(1)} %get-tuple-element.34), channel_id=1, source_target_pairs={{8,0},{16,8},{24,16},{0,24},{9,1},{17,9},{25,17},{1,25},{10,2},{18... | collective-permute-start | bytes 196616 | tf_op jit(solution)/shard_map/ppermute | solution.py:19
  88.1 6.0 %collective-permute-start.15 = (f32[64,4,1,64]{0,3,2,1:T(8,128)S(1)}, f32[64,4,1,64]{0,3,2,1:T(8,128)S(1)}, u32[]{:S(2)}, u32[]{:S(2)}) collective-permute-start(f32[64,4,1,64]{0,3,2,1:T(8,128)S(1)} %get-tuple-element.33), channel_id=1, source_target_pairs={{0,8},{8,16},{16,24},{24,0},{1,9},{9,17},{17,25},{25,1},{2,10},{10... | collective-permute-start | bytes 196616 | tf_op jit(solution)/shard_map/ppermute | solution.py:18
  88.1 9.6 %collective-permute-start.12 = (f32[64,1,4,64]{0,3,2,1:T(8,128)S(1)}, f32[64,1,4,64]{0,3,2,1:T(8,128)S(1)}, u32[]{:S(2)}, u32[]{:S(2)}) collective-permute-start(f32[64,1,4,64]{0,3,2,1:T(8,128)S(1)} %get-tuple-element.32), channel_id=1, source_target_pairs={{32,0},{64,32},{96,64},{0,96},{33,1},{65,33},{97,65},{1,97},{34,2}... | collective-permute-start | bytes 196616 | tf_op jit(solution)/shard_map/ppermute | solution.py:19
  90.5 7.1 %collective-permute-start.13 = (f32[64,1,4,64]{0,3,2,1:T(8,128)S(1)}, f32[64,1,4,64]{0,3,2,1:T(8,128)S(1)}, u32[]{:S(2)}, u32[]{:S(2)}) collective-permute-start(f32[64,1,4,64]{0,3,2,1:T(8,128)S(1)} %get-tuple-element.31), channel_id=1, source_target_pairs={{0,32},{32,64},{64,96},{96,0},{1,33},{33,65},{65,97},{97,1},{2,34}... | collective-permute-start | bytes 196616 | tf_op jit(solution)/shard_map/ppermute | solution.py:18
  90.6 4.1 %collective-permute-start.16 = (f32[64,4,4,1]{0,3,2,1:T(1,128)S(1)}, f32[64,4,4,1]{0,3,2,1:T(1,128)S(1)}, u32[]{:S(2)}, u32[]{:S(2)}) collective-permute-start(f32[64,4,4,1]{0,3,2,1:T(1,128)S(1)} %get-tuple-element.29), channel_id=1, source_target_pairs={{1,0},{2,1},{3,2},{4,3},{5,4},{6,5},{7,6},{0,7},{9,8},{10,9},{11,1... | collective-permute-start | bytes 12296 | tf_op jit(solution)/shard_map/ppermute | solution.py:19
  91.5 6.1 %collective-permute-start.17 = (f32[64,4,4,1]{0,3,2,1:T(1,128)S(1)}, f32[64,4,4,1]{0,3,2,1:T(1,128)S(1)}, u32[]{:S(2)}, u32[]{:S(2)}) collective-permute-start(f32[64,4,4,1]{0,3,2,1:T(1,128)S(1)} %get-tuple-element.30), channel_id=1, source_target_pairs={{0,1},{1,2},{2,3},{3,4},{4,5},{5,6},{6,7},{7,0},{8,9},{9,10},{10,1... | collective-permute-start | bytes 12296 | tf_op jit(solution)/shard_map/ppermute | solution.py:18
  98.1 7.2 %collective-permute-start.20 = (f32[64,4,1,64]{0,3,2,1:T(8,128)S(1)}, f32[64,4,1,64]{0,3,2,1:T(8,128)S(1)}, u32[]{:S(2)}, u32[]{:S(2)}) collective-permute-start(f32[64,4,1,64]{0,3,2,1:T(8,128)S(1)} %get-tuple-element.28), channel_id=1, source_target_pairs={{8,0},{16,8},{24,16},{0,24},{9,1},{17,9},{25,17},{1,25},{10,2},{18... | collective-permute-start | bytes 196616 | tf_op jit(solution)/shard_map/ppermute | solution.py:19
  101.1 6.7 %collective-permute-start.21 = (f32[64,4,1,64]{0,3,2,1:T(8,128)S(1)}, f32[64,4,1,64]{0,3,2,1:T(8,128)S(1)}, u32[]{:S(2)}, u32[]{:S(2)}) collective-permute-start(f32[64,4,1,64]{0,3,2,1:T(8,128)S(1)} %get-tuple-element.27), channel_id=1, source_target_pairs={{0,8},{8,16},{16,24},{24,0},{1,9},{9,17},{17,25},{25,1},{2,10},{10... | collective-permute-start | bytes 196616 | tf_op jit(solution)/shard_map/ppermute | solution.py:18
  101.2 10.2 %collective-permute-start.18 = (f32[64,1,4,64]{0,3,2,1:T(8,128)S(1)}, f32[64,1,4,64]{0,3,2,1:T(8,128)S(1)}, u32[]{:S(2)}, u32[]{:S(2)}) collective-permute-start(f32[64,1,4,64]{0,3,2,1:T(8,128)S(1)} %get-tuple-element.26), channel_id=1, source_target_pairs={{32,0},{64,32},{96,64},{0,96},{33,1},{65,33},{97,65},{1,97},{34,2}... | collective-permute-start | bytes 196616 | tf_op jit(solution)/shard_map/ppermute | solution.py:19
  104.6 6.8 %collective-permute-start.19 = (f32[64,1,4,64]{0,3,2,1:T(8,128)S(1)}, f32[64,1,4,64]{0,3,2,1:T(8,128)S(1)}, u32[]{:S(2)}, u32[]{:S(2)}) collective-permute-start(f32[64,1,4,64]{0,3,2,1:T(8,128)S(1)} %get-tuple-element.25), channel_id=1, source_target_pairs={{0,32},{32,64},{64,96},{96,0},{1,33},{33,65},{65,97},{97,1},{2,34}... | collective-permute-start | bytes 196616 | tf_op jit(solution)/shard_map/ppermute | solution.py:18
  104.8 4.0 %collective-permute-start.22 = (f32[64,4,4,1]{0,3,2,1:T(1,128)S(1)}, f32[64,4,4,1]{0,3,2,1:T(1,128)S(1)}, u32[]{:S(2)}, u32[]{:S(2)}) collective-permute-start(f32[64,4,4,1]{0,3,2,1:T(1,128)S(1)} %get-tuple-element.23), channel_id=1, source_target_pairs={{1,0},{2,1},{3,2},{4,3},{5,4},{6,5},{7,6},{0,7},{9,8},{10,9},{11,1... | collective-permute-start | bytes 12296 | tf_op jit(solution)/shard_map/ppermute | solution.py:19
  105.3 6.1 %collective-permute-start.23 = (f32[64,4,4,1]{0,3,2,1:T(1,128)S(1)}, f32[64,4,4,1]{0,3,2,1:T(1,128)S(1)}, u32[]{:S(2)}, u32[]{:S(2)}) collective-permute-start(f32[64,4,4,1]{0,3,2,1:T(1,128)S(1)} %get-tuple-element.24), channel_id=1, source_target_pairs={{0,1},{1,2},{2,3},{3,4},{4,5},{5,6},{6,7},{7,0},{8,9},{9,10},{10,1... | collective-permute-start | bytes 12296 | tf_op jit(solution)/shard_map/ppermute | solution.py:18
  112.2 7.3 %collective-permute-start.26 = (f32[64,2,1,32]{0,3,2,1:T(8,128)S(1)}, f32[64,2,1,32]{0,3,2,1:T(8,128)S(1)}, u32[]{:S(2)}, u32[]{:S(2)}) collective-permute-start(f32[64,2,1,32]{0,3,2,1:T(8,128)S(1)} %get-tuple-element.46), channel_id=1, source_target_pairs={{8,0},{16,8},{24,16},{0,24},{9,1},{17,9},{25,17},{1,25},{10,2},{18... | collective-permute-start | bytes 49160 | tf_op jit(solution)/shard_map/ppermute | solution.py:19
  114.9 7.0 %collective-permute-start.27 = (f32[64,2,1,32]{0,3,2,1:T(8,128)S(1)}, f32[64,2,1,32]{0,3,2,1:T(8,128)S(1)}, u32[]{:S(2)}, u32[]{:S(2)}) collective-permute-start(f32[64,2,1,32]{0,3,2,1:T(8,128)S(1)} %get-tuple-element.45), channel_id=1, source_target_pairs={{0,8},{8,16},{16,24},{24,0},{1,9},{9,17},{17,25},{25,1},{2,10},{10... | collective-permute-start | bytes 49160 | tf_op jit(solution)/shard_map/ppermute | solution.py:18
  114.9 10.7 %collective-permute-start.24 = (f32[64,1,2,32]{0,3,2,1:T(8,128)S(1)}, f32[64,1,2,32]{0,3,2,1:T(8,128)S(1)}, u32[]{:S(2)}, u32[]{:S(2)}) collective-permute-start(f32[64,1,2,32]{0,3,2,1:T(8,128)S(1)} %get-tuple-element.44), channel_id=1, source_target_pairs={{32,0},{64,32},{96,64},{0,96},{33,1},{65,33},{97,65},{1,97},{34,2}... | collective-permute-start | bytes 49160 | tf_op jit(solution)/shard_map/ppermute | solution.py:19
  118.8 6.8 %collective-permute-start.25 = (f32[64,1,2,32]{0,3,2,1:T(8,128)S(1)}, f32[64,1,2,32]{0,3,2,1:T(8,128)S(1)}, u32[]{:S(2)}, u32[]{:S(2)}) collective-permute-start(f32[64,1,2,32]{0,3,2,1:T(8,128)S(1)} %get-tuple-element.43), channel_id=1, source_target_pairs={{0,32},{32,64},{64,96},{96,0},{1,33},{33,65},{65,97},{97,1},{2,34}... | collective-permute-start | bytes 49160 | tf_op jit(solution)/shard_map/ppermute | solution.py:18
  119.0 3.9 %collective-permute-start.28 = (f32[64,2,2,1]{0,3,2,1:T(1,128)S(1)}, f32[64,2,2,1]{0,3,2,1:T(1,128)S(1)}, u32[]{:S(2)}, u32[]{:S(2)}) collective-permute-start(f32[64,2,2,1]{0,3,2,1:T(1,128)S(1)} %get-tuple-element.41), channel_id=1, source_target_pairs={{1,0},{2,1},{3,2},{4,3},{5,4},{6,5},{7,6},{0,7},{9,8},{10,9},{11,1... | collective-permute-start | bytes 3080 | tf_op jit(solution)/shard_map/ppermute | solution.py:19
  119.6 6.0 %collective-permute-start.29 = (f32[64,2,2,1]{0,3,2,1:T(1,128)S(1)}, f32[64,2,2,1]{0,3,2,1:T(1,128)S(1)}, u32[]{:S(2)}, u32[]{:S(2)}) collective-permute-start(f32[64,2,2,1]{0,3,2,1:T(1,128)S(1)} %get-tuple-element.42), channel_id=1, source_target_pairs={{0,1},{1,2},{2,3},{3,4},{4,5},{5,6},{6,7},{7,0},{8,9},{9,10},{10,1... | collective-permute-start | bytes 3080 | tf_op jit(solution)/shard_map/ppermute | solution.py:18
  125.7 5.8 %collective-permute-start.32 = (f32[64,2,1,32]{0,3,2,1:T(8,128)S(1)}, f32[64,2,1,32]{0,3,2,1:T(8,128)S(1)}, u32[]{:S(2)}, u32[]{:S(2)}) collective-permute-start(f32[64,2,1,32]{0,3,2,1:T(8,128)S(1)} %get-tuple-element.40), channel_id=1, source_target_pairs={{8,0},{16,8},{24,16},{0,24},{9,1},{17,9},{25,17},{1,25},{10,2},{18... | collective-permute-start | bytes 49160 | tf_op jit(solution)/shard_map/ppermute | solution.py:19
  128.5 6.0 %collective-permute-start.33 = (f32[64,2,1,32]{0,3,2,1:T(8,128)S(1)}, f32[64,2,1,32]{0,3,2,1:T(8,128)S(1)}, u32[]{:S(2)}, u32[]{:S(2)}) collective-permute-start(f32[64,2,1,32]{0,3,2,1:T(8,128)S(1)} %get-tuple-element.39), channel_id=1, source_target_pairs={{0,8},{8,16},{16,24},{24,0},{1,9},{9,17},{17,25},{25,1},{2,10},{10... | collective-permute-start | bytes 49160 | tf_op jit(solution)/shard_map/ppermute | solution.py:18
  128.5 9.1 %collective-permute-start.30 = (f32[64,1,2,32]{0,3,2,1:T(8,128)S(1)}, f32[64,1,2,32]{0,3,2,1:T(8,128)S(1)}, u32[]{:S(2)}, u32[]{:S(2)}) collective-permute-start(f32[64,1,2,32]{0,3,2,1:T(8,128)S(1)} %get-tuple-element.38), channel_id=1, source_target_pairs={{32,0},{64,32},{96,64},{0,96},{33,1},{65,33},{97,65},{1,97},{34,2}... | collective-permute-start | bytes 49160 | tf_op jit(solution)/shard_map/ppermute | solution.py:19
  131.3 6.3 %collective-permute-start.31 = (f32[64,1,2,32]{0,3,2,1:T(8,128)S(1)}, f32[64,1,2,32]{0,3,2,1:T(8,128)S(1)}, u32[]{:S(2)}, u32[]{:S(2)}) collective-permute-start(f32[64,1,2,32]{0,3,2,1:T(8,128)S(1)} %get-tuple-element.37), channel_id=1, source_target_pairs={{0,32},{32,64},{64,96},{96,0},{1,33},{33,65},{65,97},{97,1},{2,34}... | collective-permute-start | bytes 49160 | tf_op jit(solution)/shard_map/ppermute | solution.py:18
  131.5 3.9 %collective-permute-start.34 = (f32[64,2,2,1]{0,3,2,1:T(1,128)S(1)}, f32[64,2,2,1]{0,3,2,1:T(1,128)S(1)}, u32[]{:S(2)}, u32[]{:S(2)}) collective-permute-start(f32[64,2,2,1]{0,3,2,1:T(1,128)S(1)} %get-tuple-element.35), channel_id=1, source_target_pairs={{1,0},{2,1},{3,2},{4,3},{5,4},{6,5},{7,6},{0,7},{9,8},{10,9},{11,1... | collective-permute-start | bytes 3080 | tf_op jit(solution)/shard_map/ppermute | solution.py:19
  131.6 6.1 %collective-permute-start.35 = (f32[64,2,2,1]{0,3,2,1:T(1,128)S(1)}, f32[64,2,2,1]{0,3,2,1:T(1,128)S(1)}, u32[]{:S(2)}, u32[]{:S(2)}) collective-permute-start(f32[64,2,2,1]{0,3,2,1:T(1,128)S(1)} %get-tuple-element.36), channel_id=1, source_target_pairs={{0,1},{1,2},{2,3},{3,4},{4,5},{5,6},{6,7},{7,0},{8,9},{9,10},{10,1... | collective-permute-start | bytes 3080 | tf_op jit(solution)/shard_map/ppermute | solution.py:18
  138.1 6.4 %collective-permute-start.38 = (f32[64,4,1,64]{0,3,2,1:T(8,128)S(1)}, f32[64,4,1,64]{0,3,2,1:T(8,128)S(1)}, u32[]{:S(2)}, u32[]{:S(2)}) collective-permute-start(f32[64,4,1,64]{0,3,2,1:T(8,128)S(1)} %get-tuple-element.22), channel_id=1, source_target_pairs={{8,0},{16,8},{24,16},{0,24},{9,1},{17,9},{25,17},{1,25},{10,2},{18... | collective-permute-start | bytes 196616 | tf_op jit(solution)/shard_map/ppermute | solution.py:19
  141.1 6.3 %collective-permute-start.39 = (f32[64,4,1,64]{0,3,2,1:T(8,128)S(1)}, f32[64,4,1,64]{0,3,2,1:T(8,128)S(1)}, u32[]{:S(2)}, u32[]{:S(2)}) collective-permute-start(f32[64,4,1,64]{0,3,2,1:T(8,128)S(1)} %get-tuple-element.21), channel_id=1, source_target_pairs={{0,8},{8,16},{16,24},{24,0},{1,9},{9,17},{17,25},{25,1},{2,10},{10... | collective-permute-start | bytes 196616 | tf_op jit(solution)/shard_map/ppermute | solution.py:18
  141.1 9.5 %collective-permute-start.36 = (f32[64,1,4,64]{0,3,2,1:T(8,128)S(1)}, f32[64,1,4,64]{0,3,2,1:T(8,128)S(1)}, u32[]{:S(2)}, u32[]{:S(2)}) collective-permute-start(f32[64,1,4,64]{0,3,2,1:T(8,128)S(1)} %get-tuple-element.20), channel_id=1, source_target_pairs={{32,0},{64,32},{96,64},{0,96},{33,1},{65,33},{97,65},{1,97},{34,2}... | collective-permute-start | bytes 196616 | tf_op jit(solution)/shard_map/ppermute | solution.py:19
  144.2 6.4 %collective-permute-start.37 = (f32[64,1,4,64]{0,3,2,1:T(8,128)S(1)}, f32[64,1,4,64]{0,3,2,1:T(8,128)S(1)}, u32[]{:S(2)}, u32[]{:S(2)}) collective-permute-start(f32[64,1,4,64]{0,3,2,1:T(8,128)S(1)} %get-tuple-element.19), channel_id=1, source_target_pairs={{0,32},{32,64},{64,96},{96,0},{1,33},{33,65},{65,97},{97,1},{2,34}... | collective-permute-start | bytes 196616 | tf_op jit(solution)/shard_map/ppermute | solution.py:18
  144.4 4.1 %collective-permute-start.40 = (f32[64,4,4,1]{0,3,2,1:T(1,128)S(1)}, f32[64,4,4,1]{0,3,2,1:T(1,128)S(1)}, u32[]{:S(2)}, u32[]{:S(2)}) collective-permute-start(f32[64,4,4,1]{0,3,2,1:T(1,128)S(1)} %get-tuple-element.17), channel_id=1, source_target_pairs={{1,0},{2,1},{3,2},{4,3},{5,4},{6,5},{7,6},{0,7},{9,8},{10,9},{11,1... | collective-permute-start | bytes 12296 | tf_op jit(solution)/shard_map/ppermute | solution.py:19
  144.5 6.1 %collective-permute-start.41 = (f32[64,4,4,1]{0,3,2,1:T(1,128)S(1)}, f32[64,4,4,1]{0,3,2,1:T(1,128)S(1)}, u32[]{:S(2)}, u32[]{:S(2)}) collective-permute-start(f32[64,4,4,1]{0,3,2,1:T(1,128)S(1)} %get-tuple-element.18), channel_id=1, source_target_pairs={{0,1},{1,2},{2,3},{3,4},{4,5},{5,6},{6,7},{7,0},{8,9},{9,10},{10,1... | collective-permute-start | bytes 12296 | tf_op jit(solution)/shard_map/ppermute | solution.py:18
  151.5 2.2 %copy-start.1 = (f32[64,8,8,128]{0,3,2,1:T(8,128)S(1)}, f32[64,8,8,128]{0,3,2,1:T(8,128)}, u32[]{:S(2)}) copy-start(f32[64,8,8,128]{0,3,2,1:T(8,128)} %fusion.7) | copy-start | bytes 6291460
where the time goes:
time: 164 us; the launch traced here: 161 us
  starting transfers between devices  65.4 us (40%)
  waiting for transfers between devices  37.5 us (23%)
  other arithmetic  36.1 us (22%)
  local copies, waits for them, and re-layouts  21.5 us (13%)
    ppermute x21, starting transfers between devices, extended(): lax.ppermute(leading, axis, [(b, a) for a, b in up])  47.4 us
    ppermute x21, waiting for transfers between devices, extended(): lax.ppermute(last, axis, up)  22.8 us
    ppermute x21, starting transfers between devices, extended(): lax.ppermute(last, axis, up)  18.1 us
    ppermute x21, waiting for transfers between devices, extended(): lax.ppermute(leading, axis, [(b, a) for a, b in up])  14.7 us
    div x1, other arithmetic, local(): first_order = (first_image - middle * orbitals) / spread  14 us
    sub x1, other arithmetic, local(): 2.0 * (second_image - middle * first_order) / spread - orbitals  11.8 us
    reduce_sum x2, other arithmetic, restrict(): field.reshape(shape[0], shape[1] // 2, 2, shape[2] // 2, 2, shape[3] // 2...  5.15 us
    unnamed x13, local copies, waits for them, and re-layouts  5.06 us
  transfers between devices with their start and end apart: 42, of which 15 were waited for; matrix products, arithmetic and copies ran while one was open for 5% of the time, Pallas kernels for 0%

commit v1 on v0

v1 whole, which is shorter than its diff:
```python
import functools

import jax
import jax.numpy as jnp
from jax import lax
from jax.experimental import pallas as pl
from jax.experimental.pallas import tpu as pltpu
from jax.sharding import PartitionSpec as P

BANDS = 64
TILE = (8, 128)
GROUPS = 16
weight = 2.0 / 3.0

VMEM = pl.BlockSpec(memory_space=pltpu.VMEM)
SMEM = pl.BlockSpec(memory_space=pltpu.SMEM)


def shape(*dims):
    return jax.ShapeDtypeStruct(dims, jnp.float32)


def call(body, ins, outs, scratch=(), aliases=None, flops=4_000_000):
    return pl.pallas_call(
        body,
        out_shape=outs,
        in_specs=ins,
        out_specs=tuple(VMEM for _ in outs),
        scratch_shapes=scratch,
        input_output_aliases=aliases or {},
        compiler_params=pltpu.CompilerParams(vmem_limit_bytes=16 * 1024 * 1024),
        cost_estimate=pl.CostEstimate(flops=flops, bytes_accessed=4_000_000, transcendentals=0),
    )


def lanes():
    return lax.broadcasted_iota(jnp.int32, TILE, 1)


def rows():
    return lax.broadcasted_iota(jnp.int32, TILE, 0)


def lroll(v, shift):
    return pltpu.roll(v, shift, 1)


def sroll(v, shift):
    return pltpu.roll(v, shift, 0)


def plane(x):
    return pl.ds(x * 8, 8)


def nearest(lane, zp, zm, x):
    return jnp.where((lane & 1) == 0, zp[x], zm[x])


def pack_fine(orb, pot, xhi, xlo, yhi, ylo, zhi, zlo):
    lane = lanes()

    def put(carry, v, slot):
        high, low = carry
        turned = lroll(v, (2 * slot + 2) & 127)
        high = jnp.where((lane >> 1) == slot, turned, high)
        low = jnp.where((lane >> 1) == ((slot + 1) & 63), turned, low)
        return high, low

    def body(b, carry):
        done = []
        for x in range(8):
            v = orb[b, plane(x), :]
            done.append(put(carry[x], v, b))
            if x == 7:
                xhi[b] = v
            if x == 0:
                xlo[b] = v
        yhi[b] = orb[b, pl.ds(7, 8, stride=8), :]
        ylo[b] = orb[b, pl.ds(0, 8, stride=8), :]
        return tuple(done)

    zero = jnp.zeros(TILE, jnp.float32)
    carry = lax.fori_loop(0, BANDS, body, tuple((zero, zero) for _ in range(8)))
    for x in range(8):
        zhi[x] = carry[x][0]
        zlo[x] = lroll(carry[x][1], 126)
    edge = (zero, zero)
    for x in range(8):
        edge = put(edge, pot[plane(x), :], x)
    zhi[8] = edge[0]
    zlo[8] = lroll(edge[1], 126)


def star(v, x, b, get, xm, xp, ym, yp, halo, lane, row):
    left = get(x - 1) if x > 0 else xm[b]
    right = get(x + 1) if x < 7 else xp[b]
    h = lroll(halo, 127 - 2 * b)
    total = left + right
    up = jnp.where(row == 7, yp[b, pl.ds(x, 1), :], sroll(v, 7))
    down = jnp.where(row == 0, ym[b, pl.ds(x, 1), :], sroll(v, 1))
    total = total + (up + down)
    ahead = jnp.where(lane == 127, h, lroll(v, 127))
    behind = jnp.where(lane == 0, h, lroll(v, 1))
    return total + (ahead + behind)


def first_image(
    middle, inverse, orb, pot, xm, xp, ym, yp, zm, zp, first, xhi, xlo, yhi, ylo, near
):
    lane, row = lanes(), rows()
    for x in range(8):
        near[plane(x), :] = nearest(lane, zp, zm, x)

    def body(b, _):
        c, r = middle[b], inverse[b]
        get = lambda x: orb[b, plane(x), :]
        for x in range(8):
            v = get(x)
            total = star(v, x, b, get, xm, xp, ym, yp, near[plane(x), :], lane, row)
            value = (((3.0 - c) + pot[plane(x), :]) * v - 0.5 * total) * r
            first[b, plane(x), :] = value
            if x == 7:
                xhi[b] = value
            if x == 0:
                xlo[b] = value
        yhi[b] = first[b, pl.ds(7, 8, stride=8), :]
        ylo[b] = first[b, pl.ds(0, 8, stride=8), :]
        return 0

    lax.fori_loop(0, BANDS, body, 0)
    xhi[BANDS] = near[plane(7), :]
    xlo[BANDS] = near[plane(0), :]
    yhi[BANDS] = near[pl.ds(7, 8, stride=8), :]
    ylo[BANDS] = near[pl.ds(0, 8, stride=8), :]


def second_image(
    middle, inverse, lane_middle, lane_inverse, orb, pot, first, xm, xp, ym, yp, zm, zp, zhi, zlo,
    second, coarse, mhi, mlo, edge,
):
    lane, row = lanes(), rows()
    even_lane, even_row = (lane & 1) == 0, (row & 1) == 0

    cells = [nearest(lane, zp, zm, x) for x in range(8)]
    pots = nearest(lane, zp, zm, 8)
    for x in range(8):
        v = cells[x]
        outer = jnp.where(even_lane, lroll(zp[x], 127), lroll(zm[x], 1))
        inner = jnp.where(even_lane, lroll(zhi[x], 127), lroll(zlo[x], 1))
        left = cells[x - 1] if x > 0 else xm[BANDS]
        right = cells[x + 1] if x < 7 else xp[BANDS]
        up = jnp.where(row == 7, yp[BANDS, pl.ds(x, 1), :], sroll(v, 7))
        down = jnp.where(row == 0, ym[BANDS, pl.ds(x, 1), :], sroll(v, 1))
        total = (left + right) + (up + down) + (outer + inner)
        here = jnp.where(even_lane, pots[:, 2 * x : 2 * x + 1], pots[:, 2 * x + 1 : 2 * x + 2])
        edge[plane(x), :] = ((3.0 - lane_middle[...] + here) * v - 0.5 * total) * lane_inverse[...]

    def image(b, x):
        get = lambda i: first[b, plane(i), :]
        v = get(x)
        total = star(v, x, b, get, xm, xp, ym, yp, edge[plane(x), :], lane, row)
        c, r = middle[b], inverse[b]
        value = (((3.0 - c) + pot[plane(x), :]) * v - 0.5 * total) * (2.0 * r)
        value = value - orb[b, plane(x), :]
        second[b, plane(x), :] = value
        return value

    def pair_lanes(a, b):
        return jnp.where(even_lane, a + lroll(a, 127), b + lroll(b, 1))

    def pair_rows(a, b):
        return jnp.where(even_row, a + sroll(a, 7), b + sroll(b, 1))

    def group(g, _):
        odd = g & 1
        for big in range(4):
            sums = []
            for k in range(4):
                b = g * 4 + k
                sums.append(image(b, 2 * big) + image(b, 2 * big + 1))
            packed = 0.5 * pair_rows(pair_lanes(sums[0], sums[1]), pair_lanes(sums[2], sums[3]))
            coarse[g, plane(big), :] = packed
            mine = (lane >> 4) == 2 * big + odd
            at = 32 * big + 16 * odd
            half = g >> 1
            mhi[half] = jnp.where(mine, lroll(packed, (at + 16) & 127), mhi[half])
            mlo[half] = jnp.where(mine, lroll(packed, at), mlo[half])
        return 0

    sums = [pot[plane(2 * i), :] + pot[plane(2 * i + 1), :] for i in range(4)]
    packed = 0.125 * pair_rows(pair_lanes(sums[0], sums[1]), pair_lanes(sums[2], sums[3]))
    mhi[8] = packed
    mlo[8] = packed
    lax.fori_loop(0, GROUPS, group, 0)
    for g in range(GROUPS):
        coarse[g, plane(4), :] = packed


def add_halo(left, right, coarse_in, coarse):
    lane = lanes()
    first_half = ((lane >> 4) & 1) == 0
    beyond = jnp.where(lane < 64, right[8], left[8])
    for g in range(GROUPS):
        a, b = left[g // 2], right[g // 2]
        if g % 2 == 0:
            b = lroll(b, 16)
        else:
            a = lroll(a, 112)
        coarse[g, plane(5), :] = jnp.where(first_half, a, b)
        coarse[g, plane(6), :] = beyond


def coarse_solve(got, out, source, diagonal, scale, start, level, source_two, scale_two, two_a, two_b):
    lane, row = lanes(), rows()
    even_lane, even_row = (lane & 1) == 0, (row & 1) == 0
    low_lane, low_row = (lane & 2) == 0, (row & 2) == 0

    def pair_sum(v):
        v = v + jnp.where(low_row, sroll(v, 6), sroll(v, 2))
        return v + jnp.where(low_lane, lroll(v, 126), lroll(v, 2))

    def spread(v):
        a = jnp.where(even_lane, v, lroll(v, 1))
        b = jnp.where(even_lane, lroll(v, 127), v)
        out = []
        for w in (a, b):
            out.append((jnp.where(even_row, w, sroll(w, 1)), jnp.where(even_row, sroll(w, 7), w)))
        return [out[0][0], out[1][0], out[0][1], out[1][1]]

    def unpack(src, _):
        gx, gy = src >> 2, src & 3
        halo = got[src, plane(5), :]
        for t in range(2):
            pots = spread(got[src, plane(4 if t == 0 else 6), :])
            for big in range(4):
                at = (gx * 4 + big, gy * 2 + t)
                b = got[src, plane(big), :] if t == 0 else lroll(halo, 112 - 32 * big)
                d = pots[big] + 0.8
                w = weight / d
                source[at] = b
                diagonal[at] = d
                scale[at] = 0.125 * w
                start[at] = w * b
            for k in range(2):
                p = 0.125 * pair_sum(pots[2 * k] + pots[2 * k + 1])
                scale_two[gx * 2 + k, gy * 2 + t] = weight / (p + 0.2375)
        return 0

    lax.fori_loop(0, GROUPS, unpack, 0)

    def load(ref, x):
        return [[ref[x, gy * 2 + t] for t in range(2)] for gy in range(4)]

    def sides(ref, x, count, step, only=2):
        here = load(ref, x)
        before = lax.rem(x + (count - 1), count)
        after = lax.rem(x + 1, count)
        down = [[sroll(here[gy][t], step) for t in range(2)] for gy in range(4)]
        up = [[sroll(here[gy][t], 8 - step) for t in range(2)] for gy in range(4)] if step != 4 else down
        behind = [[lroll(here[gy][t], step) for t in range(2)] for gy in range(4)]
        ahead = [[lroll(here[gy][t], 128 - step) for t in range(2)] for gy in range(4)]
        totals = []
        for gy in range(4):
            line = []
            for t in range(only):
                total = ref[before, gy * 2 + t] + ref[after, gy * 2 + t]
                y = jnp.where(row < step, down[(gy + 3) % 4][t], down[gy][t])
                y = y + jnp.where(row >= 8 - step, up[(gy + 1) % 4][t], up[gy][t])
                z = jnp.where(lane < step, behind[gy][1 - t], behind[gy][t])
                z = z + jnp.where(lane >= 128 - step, ahead[gy][1 - t], ahead[gy][t])
                line.append(total + y + z)
            totals.append(line)
        return here, totals

    def sweep_one(x, _):
        here, totals = sides(start, x, 16, 2)
        for gy in range(4):
            for t in range(2):
                at = (x, gy * 2 + t)
                level[at] = (4.0 / 3.0) * here[gy][t] + scale[at] * totals[gy][t]
        return 0

    lax.fori_loop(0, 16, sweep_one, 0)

    def residue(pair, _):
        sums = [[None, None] for _ in range(4)]
        for k in range(2):
            x = 2 * pair + k
            here, totals = sides(level, x, 16, 2)
            for gy in range(4):
                for t in range(2):
                    at = (x, gy * 2 + t)
                    r = source[at] - (diagonal[at] * here[gy][t] - 0.125 * totals[gy][t])
                    sums[gy][t] = r if k == 0 else sums[gy][t] + r
        for gy in range(4):
            for t in range(2):
                at = (pair, gy * 2 + t)
                source_two[at] = scale_two[at] * (0.5 * pair_sum(sums[gy][t]))
        return 0

    lax.fori_loop(0, 8, residue, 0)

    def sweep_two(old, new):
        def body(x, _):
            here, totals = sides(old, x, 8, 4)
            for gy in range(4):
                for t in range(2):
                    at = (x, gy * 2 + t)
                    new[at] = (
                        (1.0 / 3.0) * here[gy][t]
                        + source_two[at]
                        + (0.03125 * scale_two[at]) * totals[gy][t]
                    )
            return 0

        lax.fori_loop(0, 8, body, 0)

    sweep_two(source_two, two_a)
    sweep_two(two_a, two_b)

    def correct(pair, _):
        for k in range(2):
            for i in range(8):
                at = (2 * pair + k, i)
                level[at] = level[at] + two_b[pair, i]
        return 0

    lax.fori_loop(0, 8, correct, 0)

    def last(x, _):
        here, totals = sides(level, x, 16, 2, only=1)
        gx, big = x >> 2, x & 3
        for gy in range(4):
            at = (x, gy * 2)
            value = (1.0 / 3.0) * here[gy][0] + start[at] + scale[at] * totals[gy][0]
            out[gx * 4 + gy, pl.ds(pl.multiple_of(big * 8, 8), 8), :] = value
        return 0

    lax.fori_loop(0, 16, last, 0)


def finish(second, got, out):
    lane, row = lanes(), rows()
    even_lane, even_row = (lane & 1) == 0, (row & 1) == 0

    def group(g, _):
        for big in range(4):
            v = got[g, plane(big), :]
            pair = (
                jnp.where(even_lane, v, lroll(v, 1)),
                jnp.where(even_lane, lroll(v, 127), v),
            )
            for k in range(4):
                w = pair[k % 2]
                if k < 2:
                    w = jnp.where(even_row, w, sroll(w, 1))
                else:
                    w = jnp.where(even_row, sroll(w, 7), w)
                b = g * 4 + k
                for x in (2 * big, 2 * big + 1):
                    out[b, plane(x), :] = second[b, plane(x), :] + w
        return 0

    lax.fori_loop(0, GROUPS, group, 0)


def swap(high, low, axis):
    size = lax.axis_size(axis)
    up = [(i, (i + 1) % size) for i in range(size)]
    return lax.ppermute(high, axis, up), lax.ppermute(low, axis, [(b, a) for a, b in up])


def local(orbitals, potential, centre, half_width):
    orb = orbitals.reshape(BANDS, 64, 128)
    pot = potential.reshape(64, 128)
    inverse = 1.0 / half_width
    lane_middle = jnp.repeat(centre, 2)[None]
    lane_inverse = jnp.repeat(inverse, 2)[None]
    face, wide = shape(BANDS, 8, 128), shape(BANDS + 1, 8, 128)
    thin, block = shape(9, 8, 128), shape(BANDS, 64, 128)

    xhi, xlo, yhi, ylo, zhi, zlo = call(
        pack_fine, [VMEM] * 2, (face, face, face, face, thin, thin)
    )(orb, pot)
    zm, zp = swap(zhi, zlo, "gz")
    ym, yp = swap(yhi, ylo, "gy")
    xm, xp = swap(xhi, xlo, "gx")
    first, xhi, xlo, yhi, ylo = call(
        first_image,
        [SMEM] * 2 + [VMEM] * 8,
        (block, wide, wide, wide, wide),
        scratch=(pltpu.VMEM((64, 128), jnp.float32),),
    )(centre, inverse, orb, pot, xm, xp, ym, yp, zm, zp)
    ym, yp = swap(yhi, ylo, "gy")
    xm, xp = swap(xhi, xlo, "gx")
    second, coarse, mhi, mlo = call(
        second_image,
        [SMEM] * 2 + [VMEM] * 13,
        (block, shape(GROUPS, 56, 128), thin, thin),
        scratch=(pltpu.VMEM((64, 128), jnp.float32),),
    )(centre, inverse, lane_middle, lane_inverse, orb, pot, first, xm, xp, ym, yp, zm, zp, zhi, zlo)
    left, right = swap(mhi, mlo, "gz")
    (coarse,) = call(add_halo, [VMEM] * 3, (shape(GROUPS, 56, 128),), aliases={2: 0})(
        left, right, coarse
    )
    got = lax.all_to_all(coarse, ("gx", "gy"), 0, 0, tiled=True)
    lines = pltpu.VMEM((16, 8, 8, 128), jnp.float32)
    half = pltpu.VMEM((8, 8, 8, 128), jnp.float32)
    (level,) = call(
        coarse_solve,
        [VMEM],
        (shape(GROUPS, 32, 128),),
        scratch=(lines,) * 5 + (half,) * 4,
    )(got)
    level = lax.all_to_all(level, ("gx", "gy"), 0, 0, tiled=True)
    (out,) = call(finish, [VMEM] * 2, (block,))(second, level)
    return out.reshape(BANDS, 8, 8, 128)


def solution(mesh):
    in_specs = (P(None, "gx", "gy", "gz"), P("gx", "gy", "gz"), P(), P())
    out_specs = P(None, "gx", "gy", "gz")
    return jax.shard_map(local, mesh=mesh, in_specs=in_specs, out_specs=out_specs, check_vma=False)
```

time: 164 us -> 101 us (0.62); the launches traced: 161 us -> 101 us
  starting transfers between devices: 65.4 us -> 20.1 us
  other arithmetic: 36.1 us -> 0.01 us
  Pallas kernels: 0 us -> 30.5 us
  blocking collectives: 0 us -> 28.2 us
  waiting for transfers between devices: 37.5 us -> 16.5 us
  local copies, waits for them, and re-layouts: 21.5 us -> 5.72 us
    ppermute x42 -> x12, starting transfers between devices: 65.4 us -> 20.1 us  [the longest x6 10.5 us: swap(): lax.ppermute(high, axis, up)]
    pallas_call x0 -> x6, Pallas kernels: none -> 30.5 us  [the longest x1 8.47 us: local(): call(first_image, [SMEM] * 2 + [VMEM] * 8, (block, wide, wide, wide, wide...]
    all_to_all x0 -> x2, blocking collectives: none -> 28.2 us  [the longest x1 17.5 us: local(): got = lax.all_to_all(coarse, ('gx', 'gy'), 0, 0, tiled=True)]
    ppermute x42 -> x12, waiting for transfers between devices: 37.5 us -> 16.5 us  [the longest x6 9.39 us: swap(): lax.ppermute(high, axis, up)]
    div x3 -> x1, other arithmetic: 14.3 us -> 0.01 us  [local(): inverse = 1.0 / half_width]
    sub x2 -> x0, other arithmetic: 12.1 us -> none  [the longest x1 11.8 us: local(): 2.0 * (second_image - middle * first_order) / spread - orbitals]
    slice x21 -> x0, local copies, waits for them, and re-layouts: 5.86 us -> none  [the longest x14 4.68 us: extended(): last = lax.slice_in_dim(array, length - width, length, axis=dim)]
    reduce_sum x4 -> x0, other arithmetic: 5.49 us -> none  [the longest x2 5.15 us: restrict(): field.reshape(shape[0], shape[1] // 2, 2, shape[2] // 2, 2, shape[3] // 2...]
  transfers between devices with their start and end apart: 42 -> 12, of which waited for: 15 -> 5; matrix products, arithmetic and copies ran while one was open for 5% -> 0% of each run, Pallas kernels for 0% -> 0%
where the time goes in v1:
time: 101 us
  Pallas kernels  30.5 us (30%)
  blocking collectives  28.2 us (28%)
  starting transfers between devices  20.1 us (20%)
  waiting for transfers between devices  16.5 us (16%)
  local copies, waits for them, and re-layouts  5.72 us (6%)
    all_to_all x1, blocking collectives, local(): got = lax.all_to_all(coarse, ('gx', 'gy'), 0, 0, tiled=True)  17.5 us
    all_to_all x1, blocking collectives, local(): level = lax.all_to_all(level, ('gx', 'gy'), 0, 0, tiled=True)  10.7 us
    ppermute x6, starting transfers between devices, swap(): lax.ppermute(high, axis, up)  10.5 us
    ppermute x6, starting transfers between devices, swap(): lax.ppermute(low, axis, [(b, a) for a, b in up])  9.64 us
    ppermute x6, waiting for transfers between devices, swap(): lax.ppermute(high, axis, up)  9.39 us
    pallas_call x1, Pallas kernels, local(): call(first_image, [SMEM] * 2 + [VMEM] * 8, (block, wide, wide, wide, wide...  8.47 us
    pallas_call x1, Pallas kernels, local(): call(coarse_solve, [VMEM], (shape(GROUPS, 32, 128),), scratch=(lines,) *...  8.43 us
    ppermute x6, waiting for transfers between devices, swap(): lax.ppermute(low, axis, [(b, a) for a, b in up])  7.06 us
  transfers between devices with their start and end apart: 12, of which 5 were waited for; matrix products, arithmetic and copies ran while one was open for 0% of the time, Pallas kernels for 0%

profile of v1, /device:TPU:1, one launch (start us, length us, event | category | flops | bytes accessed | tf_op | source)
XLA Modules:
  0.0 101.1 jit_solution(12361265289781328711)
XLA Ops:
  0.0 0.0 copy-start.7
  0.0 0.0 copy-start.6
  0.0 0.0 copy-start
  0.0 1.6 %copy-done = f32[64,8,8,128]{3,2,1,0:T(8,128)S(1)} copy-done((f32[64,8,8,128]{3,2,1,0:T(8,128)S(1)}, f32[64,8,8,128]{3,2,1,0:T(8,128)}, u32[]{:S(2)}) %copy-start) | copy-done | bytes 2097176
  1.6 0.0 copy-start.4
  1.6 0.8 copy-done.4
  2.4 5.0 %shard_map.46 = (f32[64,8,128]{2,1,0:T(8,128)S(1)}, f32[64,8,128]{2,1,0:T(8,128)S(1)}, f32[64,8,128]{2,1,0:T(8,128)S(1)}, f32[64,8,128]{2,1,0:T(8,128)S(1)}, f32...) custom-call(f32[64,64,128]{2,1,0:T(8,128)S(1)} %bitcast.3, f32[64,128]{1,0:T(8,128)S(1)} %bitcast.6), custom_call_target="tpu_custom_call" | custom-call | flops 4000000 | bytes 4000000 | tf_op jit(solution)/shard_map/pallas_call | solution.py:383
  7.4 0.0 copy-start.1
  7.4 0.0 copy-start.5
  7.4 2.6 %collective-permute-start = (f32[64,8,128]{2,1,0:T(8,128)S(1)}, f32[64,8,128]{2,1,0:T(8,128)S(1)}, u32[]{:S(2)}, u32[]{:S(2)}) collective-permute-start(f32[64,8,128]{2,1,0:T(8,128)S(1)} %get-tuple-element.20), channel_id=1, source_target_pairs={{0,32},{32,64},{64,96},{96,0},{1,33},{33,65},{65,97},{97,1},{2,34}... | collective-permute-start | bytes 786440 | tf_op jit(solution)/shard_map/ppermute | solution.py:371
  10.0 0.0 collective-permute-start.1
  10.0 1.3 %collective-permute-start.2 = (f32[64,8,128]{2,1,0:T(8,128)S(1)}, f32[64,8,128]{2,1,0:T(8,128)S(1)}, u32[]{:S(2)}, u32[]{:S(2)}) collective-permute-start(f32[64,8,128]{2,1,0:T(8,128)S(1)} %get-tuple-element.22), channel_id=1, source_target_pairs={{0,8},{8,16},{16,24},{24,0},{1,9},{9,17},{17,25},{25,1},{2,10},{10... | collective-permute-start | bytes 786440 | tf_op jit(solution)/shard_map/ppermute | solution.py:371
  11.3 1.4 %collective-permute-start.3 = (f32[64,8,128]{2,1,0:T(8,128)S(1)}, f32[64,8,128]{2,1,0:T(8,128)S(1)}, u32[]{:S(2)}, u32[]{:S(2)}) collective-permute-start(f32[64,8,128]{2,1,0:T(8,128)S(1)} %get-tuple-element.23), channel_id=1, source_target_pairs={{8,0},{16,8},{24,16},{0,24},{9,1},{17,9},{25,17},{1,25},{10,2},{18... | collective-permute-start | bytes 786440 | tf_op jit(solution)/shard_map/ppermute | solution.py:371
  12.8 2.5 %collective-permute-start.4 = (f32[9,8,128]{2,1,0:T(8,128)S(1)}, f32[9,8,128]{2,1,0:T(8,128)S(1)}, u32[]{:S(2)}, u32[]{:S(2)}) collective-permute-start(f32[9,8,128]{2,1,0:T(8,128)S(1)} %get-tuple-element.24.zhi), channel_id=1, source_target_pairs={{0,1},{1,2},{2,3},{3,4},{4,5},{5,6},{6,7},{7,0},{8,9},{9,10},{10,1... | collective-permute-start | bytes 110600 | tf_op jit(solution)/shard_map/ppermute | solution.py:371
  15.2 7.0 %collective-permute-done.4.zm = f32[9,8,128]{2,1,0:T(8,128)S(1)} collective-permute-done((f32[9,8,128]{2,1,0:T(8,128)S(1)}, f32[9,8,128]{2,1,0:T(8,128)S(1)}, u32[]{:S(2)}, u32[]{:S(2)}) %collective-permute-start.4) | collective-permute-done | bytes 36896 | tf_op jit(solution)/shard_map/ppermute | solution.py:371
  22.2 1.5 %collective-permute-start.5 = (f32[9,8,128]{2,1,0:T(8,128)S(1)}, f32[9,8,128]{2,1,0:T(8,128)S(1)}, u32[]{:S(2)}, u32[]{:S(2)}) collective-permute-start(f32[9,8,128]{2,1,0:T(8,128)S(1)} %get-tuple-element.25.zlo), channel_id=1, source_target_pairs={{1,0},{2,1},{3,2},{4,3},{5,4},{6,5},{7,6},{0,7},{9,8},{10,9},{11,1... | collective-permute-start | bytes 110600 | tf_op jit(solution)/shard_map/ppermute | solution.py:371
  23.7 0.0 copy-done.7
  23.7 2.8 %collective-permute-done.5.zp = f32[9,8,128]{2,1,0:T(8,128)S(1)} collective-permute-done((f32[9,8,128]{2,1,0:T(8,128)S(1)}, f32[9,8,128]{2,1,0:T(8,128)S(1)}, u32[]{:S(2)}, u32[]{:S(2)}) %collective-permute-start.5) | collective-permute-done | bytes 36896 | tf_op jit(solution)/shard_map/ppermute | solution.py:371
  26.5 0.0 collective-permute-done.xm
  26.5 0.0 collective-permute-done.1.xp
  26.5 0.0 collective-permute-done.2.ym
  26.5 0.0 collective-permute-done.3.yp
  26.5 0.0 copy-done.6
  26.5 8.5 %shard_map.47 = (f32[64,64,128]{2,1,0:T(8,128)S(1)}, f32[65,8,128]{2,1,0:T(8,128)}, f32[65,8,128]{2,1,0:T(8,128)}, f32[65,8,128]{2,1,0:T(8,128)}, f32[65,8,128]{2,1,0:T(8,128)}) custom-call(f32[64]{0:T(128)S(1)} %copy-done.6, f32[64]{0:T(128)S(1)} %broadcast_divide_fusion.inverse, f32[64,64,128]{2,1,0:T(8,128)S(1)} %bitcast.4, f32[64,128]{1,0:T(8,128)S(1)} %bitcast.7, ...), custom_call_target="tpu_custom_call" | custom-call | flops 4000000 | bytes 4000000 | tf_op jit(solution)/shard_map/pallas_call | solution.py:389
  35.0 0.0 copy-start.2
  35.0 1.3 %copy-done.2 = f32[64,64,128]{2,1,0:T(8,128)} copy-done((f32[64,64,128]{2,1,0:T(8,128)}, f32[64,64,128]{2,1,0:T(8,128)S(1)}, u32[]{:S(2)}) %copy-start.2) | copy-done | bytes 2097176
  36.3 2.8 %collective-permute-start.6 = (f32[65,8,128]{2,1,0:T(8,128)}, f32[65,8,128]{2,1,0:T(8,128)S(1)}, u32[]{:S(2)}, u32[]{:S(2)}) collective-permute-start(f32[65,8,128]{2,1,0:T(8,128)} %get-tuple-element.27), channel_id=1, source_target_pairs={{0,32},{32,64},{64,96},{96,0},{1,33},{33,65},{65,97},{97,1},{2,34}... | collective-permute-start | bytes 798728 | tf_op jit(solution)/shard_map/ppermute | solution.py:371
  39.1 0.2 collective-permute-start.7
  39.3 1.3 %collective-permute-start.8 = (f32[65,8,128]{2,1,0:T(8,128)}, f32[65,8,128]{2,1,0:T(8,128)S(1)}, u32[]{:S(2)}, u32[]{:S(2)}) collective-permute-start(f32[65,8,128]{2,1,0:T(8,128)} %get-tuple-element.29), channel_id=1, source_target_pairs={{0,8},{8,16},{16,24},{24,0},{1,9},{9,17},{17,25},{25,1},{2,10},{10... | collective-permute-start | bytes 798728 | tf_op jit(solution)/shard_map/ppermute | solution.py:371
  40.6 1.4 %collective-permute-start.9 = (f32[65,8,128]{2,1,0:T(8,128)}, f32[65,8,128]{2,1,0:T(8,128)S(1)}, u32[]{:S(2)}, u32[]{:S(2)}) collective-permute-start(f32[65,8,128]{2,1,0:T(8,128)} %get-tuple-element.30), channel_id=1, source_target_pairs={{8,0},{16,8},{24,16},{0,24},{9,1},{17,9},{25,17},{1,25},{10,2},{18... | collective-permute-start | bytes 798728 | tf_op jit(solution)/shard_map/ppermute | solution.py:371
  42.0 0.1 broadcast_in_dim.7
  42.1 0.1 broadcast_in_dim_reshape.7.lane_inverse
  42.2 0.1 broadcast_in_dim.6
  42.3 0.1 broadcast_in_dim_reshape.6.lane_middle
  42.5 1.1 %collective-permute-done.6.xm = f32[65,8,128]{2,1,0:T(8,128)S(1)} collective-permute-done((f32[65,8,128]{2,1,0:T(8,128)}, f32[65,8,128]{2,1,0:T(8,128)S(1)}, u32[]{:S(2)}, u32[]{:S(2)}) %collective-permute-start.6) | collective-permute-done | bytes 266272 | tf_op jit(solution)/shard_map/ppermute | solution.py:371
  43.5 4.3 %collective-permute-done.7.xp = f32[65,8,128]{2,1,0:T(8,128)S(1)} collective-permute-done((f32[65,8,128]{2,1,0:T(8,128)}, f32[65,8,128]{2,1,0:T(8,128)S(1)}, u32[]{:S(2)}, u32[]{:S(2)}) %collective-permute-start.7) | collective-permute-done | bytes 266272 | tf_op jit(solution)/shard_map/ppermute | solution.py:371
  47.8 0.0 collective-permute-done.8.ym
  47.8 0.0 collective-permute-done.9.yp
  47.8 0.0 copy-done.1
  47.8 0.0 copy-done.5
  47.8 0.0 copy-start.3
  47.8 1.6 %copy-done.3 = f32[64,64,128]{2,1,0:T(8,128)S(1)} copy-done((f32[64,64,128]{2,1,0:T(8,128)S(1)}, f32[64,64,128]{2,1,0:T(8,128)}, u32[]{:S(2)}) %copy-start.3) | copy-done | bytes 2097176
  49.4 5.9 %shard_map.48 = (f32[64,64,128]{2,1,0:T(8,128)S(1)}, f32[16,56,128]{2,1,0:T(8,128)S(1)}, f32[9,8,128]{2,1,0:T(8,128)S(1)}, f32[9,8,128]{2,1,0:T(8,128)S(1)}) custom-call(f32[64]{0:T(128)S(1)} %copy-done.6, f32[64]{0:T(128)S(1)} %broadcast_divide_fusion.inverse, f32[1,128]{1,0:T(1,128)S(1)} %broadcast_in_dim_reshape.6.lane_middle, ...), custom_call_target="tpu_custom_call" | custom-call | flops 4000000 | bytes 4000000 | tf_op jit(solution)/shard_map/pallas_call | solution.py:397
  55.3 0.0 collective-permute-start.10
  55.3 5.1 %collective-permute-start.11 = (f32[9,8,128]{2,1,0:T(8,128)S(1)}, f32[9,8,128]{2,1,0:T(8,128)S(1)}, u32[]{:S(2)}, u32[]{:S(2)}) collective-permute-start(f32[9,8,128]{2,1,0:T(8,128)S(1)} %get-tuple-element.33), channel_id=1, source_target_pairs={{1,0},{2,1},{3,2},{4,3},{5,4},{6,5},{7,6},{0,7},{9,8},{10,9},{11,1... | collective-permute-start | bytes 110600 | tf_op jit(solution)/shard_map/ppermute | solution.py:371
  60.4 1.3 %collective-permute-done.10.left = f32[9,8,128]{2,1,0:T(8,128)S(1)} collective-permute-done((f32[9,8,128]{2,1,0:T(8,128)S(1)}, f32[9,8,128]{2,1,0:T(8,128)S(1)}, u32[]{:S(2)}, u32[]{:S(2)}) %collective-permute-start.10) | collective-permute-done | bytes 36896 | tf_op jit(solution)/shard_map/ppermute | solution.py:371
  61.7 0.0 collective-permute-done.11.right
  61.7 0.1 shard_map.49
  61.8 17.5 %all_to_all.10.got = f32[16,56,128]{2,1,0:T(8,128)S(1)} all-to-all(f32[16,56,128]{2,1,0:T(8,128)S(1)} %shard_map.49), channel_id=1, replica_groups=mesh['gx'=4,'gy'=4,'gz'=8] {'gx','gy'}, dimensions={0} | all-to-all | bytes 917504 | tf_op jit(solution)/shard_map/all_to_all | solution.py:407
  79.3 8.4 %shard_map.50 = f32[16,32,128]{2,1,0:T(8,128)S(1)} custom-call(f32[16,56,128]{2,1,0:T(8,128)S(1)} %all_to_all.10.got), custom_call_target="tpu_custom_call" | custom-call | flops 4000000 | bytes 4000000 | tf_op jit(solution)/shard_map/pallas_call | solution.py:410
  87.8 10.7 %all_to_all.11.got = f32[16,32,128]{2,1,0:T(8,128)S(1)} all-to-all(f32[16,32,128]{2,1,0:T(8,128)S(1)} %shard_map.50), channel_id=1, replica_groups=mesh['gx'=4,'gy'=4,'gz'=8] {'gx','gy'}, dimensions={0} | all-to-all | bytes 524288 | tf_op jit(solution)/shard_map/all_to_all | solution.py:416
  98.5 2.6 %shard_map.51 = f32[64,64,128]{2,1,0:T(8,128)} custom-call(f32[64,64,128]{2,1,0:T(8,128)S(1)} %get-tuple-element.31.second, f32[16,32,128]{2,1,0:T(8,128)S(1)} %all_to_all.11.got), custom_call_target="tpu_custom_call" | custom-call | flops 4000000 | bytes 4000000 | tf_op jit(solution)/shard_map/pallas_call | solution.py:417
  (1 shorter events, 0.0 us)
Async XLA Ops:
  0.0 23.7 %copy-start.7 = (f32[64]{0:T(128)S(1)}, f32[64]{0:T(128)}, u32[]{:S(2)}) copy-start(f32[64]{0:T(128)} %param.7) | copy-start | bytes 772
  0.0 26.5 %copy-start.6 = (f32[64]{0:T(128)S(1)}, f32[64]{0:T(128)}, u32[]{:S(2)}) copy-start(f32[64]{0:T(128)} %middle.3) | copy-start | bytes 772
  0.0 1.6 %copy-start = (f32[64,8,8,128]{3,2,1,0:T(8,128)S(1)}, f32[64,8,8,128]{3,2,1,0:T(8,128)}, u32[]{:S(2)}) copy-start(f32[64,8,8,128]{3,2,1,0:T(8,128)} %param.4) | copy-start | bytes 6291460
  1.6 0.8 copy-start.4
  7.4 40.4 %copy-start.1 = (f32[64,8,8,128]{3,2,1,0:T(8,128)S(1)}, f32[64,8,8,128]{3,2,1,0:T(8,128)}, u32[]{:S(2)}) copy-start(f32[64,8,8,128]{3,2,1,0:T(8,128)} %param.4) | copy-start | bytes 6291460
  7.4 40.4 %copy-start.5 = (f32[8,8,128]{2,1,0:T(8,128)S(1)}, f32[8,8,128]{2,1,0:T(8,128)}, u32[]{:S(2)}) copy-start(f32[8,8,128]{2,1,0:T(8,128)} %param.5) | copy-start | bytes 98308
  7.4 19.1 %collective-permute-start = (f32[64,8,128]{2,1,0:T(8,128)S(1)}, f32[64,8,128]{2,1,0:T(8,128)S(1)}, u32[]{:S(2)}, u32[]{:S(2)}) collective-permute-start(f32[64,8,128]{2,1,0:T(8,128)S(1)} %get-tuple-element.20), channel_id=1, source_target_pairs={{0,32},{32,64},{64,96},{96,0},{1,33},{33,65},{65,97},{97,1},{2,34}... | collective-permute-start | bytes 786440 | tf_op jit(solution)/shard_map/ppermute | solution.py:371
  10.0 16.5 %collective-permute-start.1 = (f32[64,8,128]{2,1,0:T(8,128)S(1)}, f32[64,8,128]{2,1,0:T(8,128)S(1)}, u32[]{:S(2)}, u32[]{:S(2)}) collective-permute-start(f32[64,8,128]{2,1,0:T(8,128)S(1)} %get-tuple-element.21), channel_id=1, source_target_pairs={{32,0},{64,32},{96,64},{0,96},{33,1},{65,33},{97,65},{1,97},{34,2}... | collective-permute-start | bytes 786440 | tf_op jit(solution)/shard_map/ppermute | solution.py:371
  10.0 16.5 %collective-permute-start.2 = (f32[64,8,128]{2,1,0:T(8,128)S(1)}, f32[64,8,128]{2,1,0:T(8,128)S(1)}, u32[]{:S(2)}, u32[]{:S(2)}) collective-permute-start(f32[64,8,128]{2,1,0:T(8,128)S(1)} %get-tuple-element.22), channel_id=1, source_target_pairs={{0,8},{8,16},{16,24},{24,0},{1,9},{9,17},{17,25},{25,1},{2,10},{10... | collective-permute-start | bytes 786440 | tf_op jit(solution)/shard_map/ppermute | solution.py:371
  11.3 15.2 %collective-permute-start.3 = (f32[64,8,128]{2,1,0:T(8,128)S(1)}, f32[64,8,128]{2,1,0:T(8,128)S(1)}, u32[]{:S(2)}, u32[]{:S(2)}) collective-permute-start(f32[64,8,128]{2,1,0:T(8,128)S(1)} %get-tuple-element.23), channel_id=1, source_target_pairs={{8,0},{16,8},{24,16},{0,24},{9,1},{17,9},{25,17},{1,25},{10,2},{18... | collective-permute-start | bytes 786440 | tf_op jit(solution)/shard_map/ppermute | solution.py:371
  12.8 9.4 %collective-permute-start.4 = (f32[9,8,128]{2,1,0:T(8,128)S(1)}, f32[9,8,128]{2,1,0:T(8,128)S(1)}, u32[]{:S(2)}, u32[]{:S(2)}) collective-permute-start(f32[9,8,128]{2,1,0:T(8,128)S(1)} %get-tuple-element.24.zhi), channel_id=1, source_target_pairs={{0,1},{1,2},{2,3},{3,4},{4,5},{5,6},{6,7},{7,0},{8,9},{9,10},{10,1... | collective-permute-start | bytes 110600 | tf_op jit(solution)/shard_map/ppermute | solution.py:371
  22.2 4.3 %collective-permute-start.5 = (f32[9,8,128]{2,1,0:T(8,128)S(1)}, f32[9,8,128]{2,1,0:T(8,128)S(1)}, u32[]{:S(2)}, u32[]{:S(2)}) collective-permute-start(f32[9,8,128]{2,1,0:T(8,128)S(1)} %get-tuple-element.25.zlo), channel_id=1, source_target_pairs={{1,0},{2,1},{3,2},{4,3},{5,4},{6,5},{7,6},{0,7},{9,8},{10,9},{11,1... | collective-permute-start | bytes 110600 | tf_op jit(solution)/shard_map/ppermute | solution.py:371
  35.0 1.3 %copy-start.2 = (f32[64,64,128]{2,1,0:T(8,128)}, f32[64,64,128]{2,1,0:T(8,128)S(1)}, u32[]{:S(2)}) copy-start(f32[64,64,128]{2,1,0:T(8,128)S(1)} %get-tuple-element.26.first) | copy-start | bytes 6291460
  36.3 7.2 %collective-permute-start.6 = (f32[65,8,128]{2,1,0:T(8,128)}, f32[65,8,128]{2,1,0:T(8,128)S(1)}, u32[]{:S(2)}, u32[]{:S(2)}) collective-permute-start(f32[65,8,128]{2,1,0:T(8,128)} %get-tuple-element.27), channel_id=1, source_target_pairs={{0,32},{32,64},{64,96},{96,0},{1,33},{33,65},{65,97},{97,1},{2,34}... | collective-permute-start | bytes 798728 | tf_op jit(solution)/shard_map/ppermute | solution.py:371
  39.1 8.7 %collective-permute-start.7 = (f32[65,8,128]{2,1,0:T(8,128)}, f32[65,8,128]{2,1,0:T(8,128)S(1)}, u32[]{:S(2)}, u32[]{:S(2)}) collective-permute-start(f32[65,8,128]{2,1,0:T(8,128)} %get-tuple-element.28), channel_id=1, source_target_pairs={{32,0},{64,32},{96,64},{0,96},{33,1},{65,33},{97,65},{1,97},{34,2}... | collective-permute-start | bytes 798728 | tf_op jit(solution)/shard_map/ppermute | solution.py:371
  39.3 8.5 %collective-permute-start.8 = (f32[65,8,128]{2,1,0:T(8,128)}, f32[65,8,128]{2,1,0:T(8,128)S(1)}, u32[]{:S(2)}, u32[]{:S(2)}) collective-permute-start(f32[65,8,128]{2,1,0:T(8,128)} %get-tuple-element.29), channel_id=1, source_target_pairs={{0,8},{8,16},{16,24},{24,0},{1,9},{9,17},{17,25},{25,1},{2,10},{10... | collective-permute-start | bytes 798728 | tf_op jit(solution)/shard_map/ppermute | solution.py:371
  40.6 7.2 %collective-permute-start.9 = (f32[65,8,128]{2,1,0:T(8,128)}, f32[65,8,128]{2,1,0:T(8,128)S(1)}, u32[]{:S(2)}, u32[]{:S(2)}) collective-permute-start(f32[65,8,128]{2,1,0:T(8,128)} %get-tuple-element.30), channel_id=1, source_target_pairs={{8,0},{16,8},{24,16},{0,24},{9,1},{17,9},{25,17},{1,25},{10,2},{18... | collective-permute-start | bytes 798728 | tf_op jit(solution)/shard_map/ppermute | solution.py:371
  47.8 1.6 %copy-start.3 = (f32[64,64,128]{2,1,0:T(8,128)S(1)}, f32[64,64,128]{2,1,0:T(8,128)}, u32[]{:S(2)}) copy-start(f32[64,64,128]{2,1,0:T(8,128)} %copy-done.2) | copy-start | bytes 6291460
  55.3 6.4 %collective-permute-start.10 = (f32[9,8,128]{2,1,0:T(8,128)S(1)}, f32[9,8,128]{2,1,0:T(8,128)S(1)}, u32[]{:S(2)}, u32[]{:S(2)}) collective-permute-start(f32[9,8,128]{2,1,0:T(8,128)S(1)} %get-tuple-element.32), channel_id=1, source_target_pairs={{0,1},{1,2},{2,3},{3,4},{4,5},{5,6},{6,7},{7,0},{8,9},{9,10},{10,1... | collective-permute-start | bytes 110600 | tf_op jit(solution)/shard_map/ppermute | solution.py:371
  55.3 6.4 %collective-permute-start.11 = (f32[9,8,128]{2,1,0:T(8,128)S(1)}, f32[9,8,128]{2,1,0:T(8,128)S(1)}, u32[]{:S(2)}, u32[]{:S(2)}) collective-permute-start(f32[9,8,128]{2,1,0:T(8,128)S(1)} %get-tuple-element.33), channel_id=1, source_target_pairs={{1,0},{2,1},{3,2},{4,3},{5,4},{6,5},{7,6},{0,7},{9,8},{10,9},{11,1... | collective-permute-start | bytes 110600 | tf_op jit(solution)/shard_map/ppermute | solution.py:371
